TPU v7x, 256 devices: a whole 4x4x8 slice. The times are simulated.
256 devices in a mesh: rows: 64 (over y, z, core), rep: 4 (over x).
Axes of the slice: x: 4, y: 4, z: 8, core: 2. Of those that a mesh axis runs over, the one named last changes fastest.
Arguments:
- binned: int32 [65536, 1024], P('rows', 'rep'), may hold values from 0 to 127
- gradients: bfloat16 [65536], P('rows'), may hold values from -3 to 3
- hessians: bfloat16 [65536], P('rows'), may hold values from 0.019897461 to 0.25
- parents: int32 [65536], P('rows'), may hold values from 0 to 15
- split_feature: int32 [16], replicated, may hold values from 0 to 1023
- split_bin: int32 [16], replicated, may hold values from 32 to 95
- elected: int32 [32, 512], P(None, 'rep'), may hold values from 0 to 255
Outputs:
- new_nodes: int32 [65536], P('rows')
- best_gain: float32 [32, 4, 128], P(None, 'rep', 'rows')
- node_best: float32 [32], replicated
All inputs are finite; a program needn't handle non-finite values.
Results may differ from a plain program's by a relative error of at most 0.0003.
Values sent between devices are 32-bit elements; how exact they have to be, the bound alone decides.
A program may use at most 64 MiB of HBM per device.

v0:
```python
import math

import jax
import jax.numpy as jnp
from jax import lax
from jax.sharding import Mesh
from jax.sharding import PartitionSpec as P

BINS = 128
ROWS = ("rows_0", "rows_1", "rows_2")
ROWS_REP = ("rows_0", "rows_1", "rows_2", "rep")


l2_penalty = 1.0


def sent_to_all(shard, axis):
    copies = jnp.broadcast_to(shard, (lax.axis_size(axis), *shard.shape))
    return lax.all_to_all(copies, axis, split_axis=0, concat_axis=0, tiled=True)


def taken_together(shard, axis):
    return sent_to_all(shard, axis).max(axis=0)


def by_axis(shard, axes):
    for axis in axes:
        shard = lax.pmax(shard, axis)
    return shard


def body(binned, gradients, hessians, parents, split_feature, split_bin, elected):
    rows_here, block_width = binned.shape
    node_count, slots_here = elected.shape
    parent_count = split_feature.shape[0]
    rep_index = lax.axis_index("rep")
    parent_hot = parents[:, None] == jnp.arange(parent_count, dtype=jnp.int32)[None, :]
    row_feature = jnp.sum(jnp.where(parent_hot, split_feature[None, :], 0), axis=1)
    row_bin = jnp.sum(jnp.where(parent_hot, split_bin[None, :], 0), axis=1)
    local_col = row_feature - rep_index * block_width
    column_hot = local_col[:, None] == jnp.arange(block_width, dtype=jnp.int32)[None, :]
    owned_value = jnp.sum(jnp.where(column_hot, binned, 0), axis=1)
    owned_mask = (local_col >= 0) & (local_col < block_width)
    side_here = jnp.where(owned_mask & (owned_value > row_bin), 1, 0).astype(jnp.int32)
    side_bits = taken_together(side_here, "rep")
    new_nodes = 2 * parents + side_bits
    node_hot = new_nodes[:, None] == jnp.arange(node_count, dtype=jnp.int32)[None, :]
    nothing = jnp.zeros((), jnp.bfloat16)
    weights = jnp.concatenate(
        [
            jnp.where(node_hot, gradients[:, None], nothing),
            jnp.where(node_hot, hessians[:, None], nothing),
        ],
        axis=1,
    )
    feature_block = math.gcd(block_width, max(1, 8192 // BINS))
    block_count = block_width // feature_block
    row_block = math.gcd(rows_here, max(8, 2**22 // (feature_block * BINS)))
    row_count = rows_here // row_block
    bin_ids = jnp.arange(BINS, dtype=jnp.int32)
    blocks = jnp.transpose(
        binned.reshape(row_count, row_block, block_count, feature_block), (2, 0, 1, 3)
    )
    weight_blocks = weights.reshape(row_count, row_block, 2 * node_count)

    def build_block(unused, columns):

        def add_rows(total, pair):
            piece, weight_piece = pair
            one_hot = (piece[:, :, None] == bin_ids[None, None, :]).astype(jnp.bfloat16)
            one_hot = one_hot.reshape(row_block, feature_block * BINS)
            partial_value = lax.dot_general(
                weight_piece, one_hot, (((0,), (0,)), ((), ())), preferred_element_type=jnp.float32
            )
            return (total + partial_value, None)

        start = jnp.zeros((2 * node_count, feature_block * BINS), jnp.float32)
        summed_rows, _ = lax.scan(add_rows, start, (columns, weight_blocks))
        return (unused, summed_rows)

    _, block_sums = lax.scan(build_block, 0, blocks)
    block_sums = block_sums.reshape(block_count, 2, node_count, feature_block, BINS)
    block_of = (elected // feature_block)[None, :, :]
    inner_of = (elected % feature_block)[None, :, :]
    channel = jnp.arange(2, dtype=jnp.int32)[:, None, None]
    node_of = jnp.arange(node_count, dtype=jnp.int32)[None, :, None]
    selected = block_sums[block_of, channel, node_of, inner_of]
    row_devices = lax.axis_size(ROWS)
    owned_slots = slots_here // row_devices
    sectioned = selected.reshape(2, node_count, row_devices, owned_slots, BINS)
    arrived = lax.all_to_all(sectioned, ROWS, split_axis=2, concat_axis=2, tiled=True)
    summed = jnp.sum(arrived, axis=2)
    totals = jnp.sum(summed, axis=3)
    total_grad = totals[0][:, :, None]
    total_hess = totals[1][:, :, None]
    left_sums = jnp.cumsum(summed, axis=3)[:, :, :, :-1]
    left_grad = left_sums[0]
    left_hess = left_sums[1]
    split_gain = 0.5 * (
        left_grad * left_grad / (left_hess + l2_penalty)
        + (total_grad - left_grad) ** 2 / (total_hess - left_hess + l2_penalty)
        - total_grad * total_grad / (total_hess + l2_penalty)
    )
    best_slot = jnp.max(split_gain, axis=2)
    node_local = jnp.max(best_slot, axis=1)
    node_best = by_axis(node_local, ROWS_REP)
    return (new_nodes, best_slot[:, None, :], node_best)


def solution(mesh):
    finer = Mesh(
        mesh.devices.reshape(4, 8, 2, mesh.shape["rep"]), ("rows_0", "rows_1", "rows_2", "rep")
    )
    placed = (P(ROWS, "rep"), P(ROWS), P(ROWS), P(ROWS), P(), P(), P(None, "rep"))
    return jax.shard_map(
        body,
        mesh=finer,
        in_specs=placed,
        out_specs=(P(ROWS), P(None, "rep", ROWS), P()),
        check_vma=False,
    )
```

profile of v0, /device:TPU:1, one launch (start us, length us, event | category | flops | bytes accessed | tf_op | source)
XLA Modules:
  0.0 415.7 jit_solution(425915785876418775)
XLA Ops:
  0.6 0.8 select_reduce_fusion.1
  1.5 1.6 select_reduce_fusion
  3.7 4.8 %all-to-all-start = ((s32[4,1,1024]{2,1,0:T(1,128)}), s32[4,1,1024]{2,1,0:T(1,128)S(1)}, u32[]{:S(2)}, u32[]{:S(2)}) async-start(s32[4,1,1024]{2,1,0:T(1,128)} %broadcast_in_dim.104), calls=%async_computation | async-start | bytes 32768 | tf_op jit(solution)/shard_map/all_to_all | solution.py:19
  8.5 0.7 fusion.14
  9.3 1.6 copy.29
  10.9 0.7 broadcast_in_dim.106
  11.6 0.7 broadcast_in_dim.109
  12.3 1.9 reshape.132
  14.9 104.7 %while.24 = (s32[]{:T(128)}, f32[4,64,8192]{2,1,0:T(8,128)}, s32[4,2,512,64]{2,1,3,0:T(2,128)}, bf16[2,512,64]{2,1,0:T(8,128)(2,1)S(1)}, s32[]{:T(128)}, /*index=5*/s32[]{:T(128)}, s32[]{:T(128)}, s32[]{:T(128)}) while((s32[]{:T(128)}, f32[4,64,8192]{2,1,0:T(8,128)}, s32[4,2,512,64]{2,1,3,0:T(2,128)}, ...), condition=%wide.region_7.8_spmd.clone, body=%wide.region_4.7_spmd.clone.sunk | while | flops 542113792 | bytes 18351864 | solution.py:81
  14.9 1.0 constant_dynamic-slice_fusion.2
  16.2 23.5 %while.25 = (s32[]{:T(128)}, f32[64,8192]{1,0:T(8,128)S(1)}, bf16[2,512,64]{2,1,0:T(8,128)(2,1)S(1)}, s32[2,512,64]{2,1,0:T(8,128)S(1)}, s32[128]{0:T(128)S(1)}, /*index=5*/s32[]{:T(128)}, s32[]{:T(128)}) while((s32[]{:T(128)}, f32[64,8192]{1,0:T(8,128)S(1)}, bf16[2,512,64]{2,1,0:T(8,128)(2,1)S(1)}, s32[2,512,64]{2,1,0:T(8,128)S(1)}, ...), condition=%wide.region_6.6_spmd.clone, body=%wide.region_5.5_spmd.clone.sunk | while | flops 542113792 | bytes 13107807 | solution.py:78
  16.2 6.4 %broadcast_compare_fusion.2 = pred[512,64,128]{2,1,0:T(32,128)(4,1)} fusion(s32[128]{0:T(128)S(1)} %get-tuple-element.225, s32[512,64]{1,0:T(8,128)S(1)} %dynamic-slice_bitcast_fusion.2), kind=kLoop, calls=%fused_computation.6.clone.1 | loop fusion | flops 4194304 | bytes 4325888 | tf_op jit(solution)/shard_map/while/body/eval_jaxpr/while/body/eval_jaxpr/eq | solution.py:70
  22.7 5.2 %fusion.27 = f32[64,8192]{1,0:T(8,128)S(1)} fusion(pred[64,8,64,128]{3,2,1,0:T(32,128)(4,1)} %bitcast.48, f32[64,8192]{1,0:T(8,128)S(1)} %get-tuple-element.215, pred[]{:T(512)S(6)} %compare.6, bf16[2,512,64]{2,1,0:T(8,128)(2,1)S(1)} %get-tuple-element.223, s32[]{:T(128)} %get-tuple-element.214), kind=kOutput, calls=%fused_computation.5.clone.1 | convolution fusion | flops 537919488 | bytes 8519685 | tf_op jit(solution)/shard_map/while/body/eval_jaxpr/while/body/eval_jaxpr/dot_general | solution.py:72
  27.9 6.4 %broadcast_compare_fusion.2 = pred[512,64,128]{2,1,0:T(32,128)(4,1)} fusion(s32[128]{0:T(128)S(1)} %get-tuple-element.225, s32[512,64]{1,0:T(8,128)S(1)} %dynamic-slice_bitcast_fusion.2), kind=kLoop, calls=%fused_computation.6.clone.1 | loop fusion | flops 4194304 | bytes 4325888 | tf_op jit(solution)/shard_map/while/body/eval_jaxpr/while/body/eval_jaxpr/eq | solution.py:70
  34.4 5.2 %fusion.27 = f32[64,8192]{1,0:T(8,128)S(1)} fusion(pred[64,8,64,128]{3,2,1,0:T(32,128)(4,1)} %bitcast.48, f32[64,8192]{1,0:T(8,128)S(1)} %get-tuple-element.215, pred[]{:T(512)S(6)} %compare.6, bf16[2,512,64]{2,1,0:T(8,128)(2,1)S(1)} %get-tuple-element.223, s32[]{:T(128)} %get-tuple-element.214), kind=kOutput, calls=%fused_computation.5.clone.1 | convolution fusion | flops 537919488 | bytes 8519685 | tf_op jit(solution)/shard_map/while/body/eval_jaxpr/while/body/eval_jaxpr/dot_general | solution.py:72
  39.6 1.5 bitcast_dynamic-update-slice_fusion.2
  41.1 1.0 constant_dynamic-slice_fusion.2
  42.3 23.5 %while.25 = (s32[]{:T(128)}, f32[64,8192]{1,0:T(8,128)S(1)}, bf16[2,512,64]{2,1,0:T(8,128)(2,1)S(1)}, s32[2,512,64]{2,1,0:T(8,128)S(1)}, s32[128]{0:T(128)S(1)}, /*index=5*/s32[]{:T(128)}, s32[]{:T(128)}) while((s32[]{:T(128)}, f32[64,8192]{1,0:T(8,128)S(1)}, bf16[2,512,64]{2,1,0:T(8,128)(2,1)S(1)}, s32[2,512,64]{2,1,0:T(8,128)S(1)}, ...), condition=%wide.region_6.6_spmd.clone, body=%wide.region_5.5_spmd.clone.sunk | while | flops 542113792 | bytes 13107807 | solution.py:78
  42.4 6.4 %broadcast_compare_fusion.2 = pred[512,64,128]{2,1,0:T(32,128)(4,1)} fusion(s32[128]{0:T(128)S(1)} %get-tuple-element.225, s32[512,64]{1,0:T(8,128)S(1)} %dynamic-slice_bitcast_fusion.2), kind=kLoop, calls=%fused_computation.6.clone.1 | loop fusion | flops 4194304 | bytes 4325888 | tf_op jit(solution)/shard_map/while/body/eval_jaxpr/while/body/eval_jaxpr/eq | solution.py:70
  48.8 5.2 %fusion.27 = f32[64,8192]{1,0:T(8,128)S(1)} fusion(pred[64,8,64,128]{3,2,1,0:T(32,128)(4,1)} %bitcast.48, f32[64,8192]{1,0:T(8,128)S(1)} %get-tuple-element.215, pred[]{:T(512)S(6)} %compare.6, bf16[2,512,64]{2,1,0:T(8,128)(2,1)S(1)} %get-tuple-element.223, s32[]{:T(128)} %get-tuple-element.214), kind=kOutput, calls=%fused_computation.5.clone.1 | convolution fusion | flops 537919488 | bytes 8519685 | tf_op jit(solution)/shard_map/while/body/eval_jaxpr/while/body/eval_jaxpr/dot_general | solution.py:72
  54.1 6.4 %broadcast_compare_fusion.2 = pred[512,64,128]{2,1,0:T(32,128)(4,1)} fusion(s32[128]{0:T(128)S(1)} %get-tuple-element.225, s32[512,64]{1,0:T(8,128)S(1)} %dynamic-slice_bitcast_fusion.2), kind=kLoop, calls=%fused_computation.6.clone.1 | loop fusion | flops 4194304 | bytes 4325888 | tf_op jit(solution)/shard_map/while/body/eval_jaxpr/while/body/eval_jaxpr/eq | solution.py:70
  60.6 5.2 %fusion.27 = f32[64,8192]{1,0:T(8,128)S(1)} fusion(pred[64,8,64,128]{3,2,1,0:T(32,128)(4,1)} %bitcast.48, f32[64,8192]{1,0:T(8,128)S(1)} %get-tuple-element.215, pred[]{:T(512)S(6)} %compare.6, bf16[2,512,64]{2,1,0:T(8,128)(2,1)S(1)} %get-tuple-element.223, s32[]{:T(128)} %get-tuple-element.214), kind=kOutput, calls=%fused_computation.5.clone.1 | convolution fusion | flops 537919488 | bytes 8519685 | tf_op jit(solution)/shard_map/while/body/eval_jaxpr/while/body/eval_jaxpr/dot_general | solution.py:72
  65.8 1.5 bitcast_dynamic-update-slice_fusion.2
  67.3 1.0 constant_dynamic-slice_fusion.2
  68.5 23.5 %while.25 = (s32[]{:T(128)}, f32[64,8192]{1,0:T(8,128)S(1)}, bf16[2,512,64]{2,1,0:T(8,128)(2,1)S(1)}, s32[2,512,64]{2,1,0:T(8,128)S(1)}, s32[128]{0:T(128)S(1)}, /*index=5*/s32[]{:T(128)}, s32[]{:T(128)}) while((s32[]{:T(128)}, f32[64,8192]{1,0:T(8,128)S(1)}, bf16[2,512,64]{2,1,0:T(8,128)(2,1)S(1)}, s32[2,512,64]{2,1,0:T(8,128)S(1)}, ...), condition=%wide.region_6.6_spmd.clone, body=%wide.region_5.5_spmd.clone.sunk | while | flops 542113792 | bytes 13107807 | solution.py:78
  68.5 6.4 %broadcast_compare_fusion.2 = pred[512,64,128]{2,1,0:T(32,128)(4,1)} fusion(s32[128]{0:T(128)S(1)} %get-tuple-element.225, s32[512,64]{1,0:T(8,128)S(1)} %dynamic-slice_bitcast_fusion.2), kind=kLoop, calls=%fused_computation.6.clone.1 | loop fusion | flops 4194304 | bytes 4325888 | tf_op jit(solution)/shard_map/while/body/eval_jaxpr/while/body/eval_jaxpr/eq | solution.py:70
  75.0 5.2 %fusion.27 = f32[64,8192]{1,0:T(8,128)S(1)} fusion(pred[64,8,64,128]{3,2,1,0:T(32,128)(4,1)} %bitcast.48, f32[64,8192]{1,0:T(8,128)S(1)} %get-tuple-element.215, pred[]{:T(512)S(6)} %compare.6, bf16[2,512,64]{2,1,0:T(8,128)(2,1)S(1)} %get-tuple-element.223, s32[]{:T(128)} %get-tuple-element.214), kind=kOutput, calls=%fused_computation.5.clone.1 | convolution fusion | flops 537919488 | bytes 8519685 | tf_op jit(solution)/shard_map/while/body/eval_jaxpr/while/body/eval_jaxpr/dot_general | solution.py:72
  80.3 6.4 %broadcast_compare_fusion.2 = pred[512,64,128]{2,1,0:T(32,128)(4,1)} fusion(s32[128]{0:T(128)S(1)} %get-tuple-element.225, s32[512,64]{1,0:T(8,128)S(1)} %dynamic-slice_bitcast_fusion.2), kind=kLoop, calls=%fused_computation.6.clone.1 | loop fusion | flops 4194304 | bytes 4325888 | tf_op jit(solution)/shard_map/while/body/eval_jaxpr/while/body/eval_jaxpr/eq | solution.py:70
  86.7 5.2 %fusion.27 = f32[64,8192]{1,0:T(8,128)S(1)} fusion(pred[64,8,64,128]{3,2,1,0:T(32,128)(4,1)} %bitcast.48, f32[64,8192]{1,0:T(8,128)S(1)} %get-tuple-element.215, pred[]{:T(512)S(6)} %compare.6, bf16[2,512,64]{2,1,0:T(8,128)(2,1)S(1)} %get-tuple-element.223, s32[]{:T(128)} %get-tuple-element.214), kind=kOutput, calls=%fused_computation.5.clone.1 | convolution fusion | flops 537919488 | bytes 8519685 | tf_op jit(solution)/shard_map/while/body/eval_jaxpr/while/body/eval_jaxpr/dot_general | solution.py:72
  91.9 1.5 bitcast_dynamic-update-slice_fusion.2
  93.4 1.0 constant_dynamic-slice_fusion.2
  94.6 23.5 %while.25 = (s32[]{:T(128)}, f32[64,8192]{1,0:T(8,128)S(1)}, bf16[2,512,64]{2,1,0:T(8,128)(2,1)S(1)}, s32[2,512,64]{2,1,0:T(8,128)S(1)}, s32[128]{0:T(128)S(1)}, /*index=5*/s32[]{:T(128)}, s32[]{:T(128)}) while((s32[]{:T(128)}, f32[64,8192]{1,0:T(8,128)S(1)}, bf16[2,512,64]{2,1,0:T(8,128)(2,1)S(1)}, s32[2,512,64]{2,1,0:T(8,128)S(1)}, ...), condition=%wide.region_6.6_spmd.clone, body=%wide.region_5.5_spmd.clone.sunk | while | flops 542113792 | bytes 13107807 | solution.py:78
  94.7 6.4 %broadcast_compare_fusion.2 = pred[512,64,128]{2,1,0:T(32,128)(4,1)} fusion(s32[128]{0:T(128)S(1)} %get-tuple-element.225, s32[512,64]{1,0:T(8,128)S(1)} %dynamic-slice_bitcast_fusion.2), kind=kLoop, calls=%fused_computation.6.clone.1 | loop fusion | flops 4194304 | bytes 4325888 | tf_op jit(solution)/shard_map/while/body/eval_jaxpr/while/body/eval_jaxpr/eq | solution.py:70
  101.1 5.2 %fusion.27 = f32[64,8192]{1,0:T(8,128)S(1)} fusion(pred[64,8,64,128]{3,2,1,0:T(32,128)(4,1)} %bitcast.48, f32[64,8192]{1,0:T(8,128)S(1)} %get-tuple-element.215, pred[]{:T(512)S(6)} %compare.6, bf16[2,512,64]{2,1,0:T(8,128)(2,1)S(1)} %get-tuple-element.223, s32[]{:T(128)} %get-tuple-element.214), kind=kOutput, calls=%fused_computation.5.clone.1 | convolution fusion | flops 537919488 | bytes 8519685 | tf_op jit(solution)/shard_map/while/body/eval_jaxpr/while/body/eval_jaxpr/dot_general | solution.py:72
  106.4 6.4 %broadcast_compare_fusion.2 = pred[512,64,128]{2,1,0:T(32,128)(4,1)} fusion(s32[128]{0:T(128)S(1)} %get-tuple-element.225, s32[512,64]{1,0:T(8,128)S(1)} %dynamic-slice_bitcast_fusion.2), kind=kLoop, calls=%fused_computation.6.clone.1 | loop fusion | flops 4194304 | bytes 4325888 | tf_op jit(solution)/shard_map/while/body/eval_jaxpr/while/body/eval_jaxpr/eq | solution.py:70
  112.9 5.2 %fusion.27 = f32[64,8192]{1,0:T(8,128)S(1)} fusion(pred[64,8,64,128]{3,2,1,0:T(32,128)(4,1)} %bitcast.48, f32[64,8192]{1,0:T(8,128)S(1)} %get-tuple-element.215, pred[]{:T(512)S(6)} %compare.6, bf16[2,512,64]{2,1,0:T(8,128)(2,1)S(1)} %get-tuple-element.223, s32[]{:T(128)} %get-tuple-element.214), kind=kOutput, calls=%fused_computation.5.clone.1 | convolution fusion | flops 537919488 | bytes 8519685 | tf_op jit(solution)/shard_map/while/body/eval_jaxpr/while/body/eval_jaxpr/dot_general | solution.py:72
  118.1 1.5 bitcast_dynamic-update-slice_fusion.2
  119.6 8.2 %copy.44 = f32[32,8,64,128]{3,2,1,0:T(8,128)} copy(f32[32,8,64,128]{3,1,2,0:T(8,128)} %bitcast.53) | data formatting | bytes 16777216
  127.8 133.7 %gather_fusion = f32[8192,128]{1,0:T(8,128)} fusion(f32[4,2,32,64,128]{4,3,2,1,0:T(8,128)} %bitcast.50, s32[8192]{0:T(1024)S(1)} %bitcast.49), kind=kCustom, calls=%fused_computation | custom fusion | bytes 8519680 | tf_op jit(solution)/shard_map/gather | solution.py:87
  261.5 4.6 %copy.31 = f32[2,32,64,2,128]{4,3,1,0,2:T(2,128)S(1)} copy(f32[2,32,64,2,128]{4,3,2,1,0:T(2,128)} %bitcast.52) | data formatting | bytes 8388608 | tf_op jit(solution)/shard_map/reshape | solution.py:90
  266.1 108.6 %all_to_all.11 = f32[2,32,64,2,128]{4,3,1,0,2:T(2,128)S(1)} all-to-all(f32[2,32,64,2,128]{4,3,1,0,2:T(2,128)S(1)} %copy.31), channel_id=1, replica_groups=mesh['rows_0'=4,'rows_1'=8,'rows_2'=2,'rep'=4] {'rows_0','rows_1','rows_2'}, dimensions={2} | all-to-all | bytes 8388608 | tf_op jit(solution)/shard_map/all_to_all | solution.py:91
  374.7 2.1 fusion.19
  377.0 1.2 reduce_window_sum.11
  378.1 0.8 fusion.20
  378.9 8.4 %pmax.28 = f32[32]{0:T(128)S(1)} all-reduce(f32[32]{0:T(128)S(1)} %get-tuple-element.110), channel_id=1, replica_groups=mesh['rows_0'=4,'rows_1'=8,'rows_2'=2,'rep'=4] {'rows_0'}, use_global_device_ids=true, to_apply=%region_13.14 | all-reduce | flops 32 | bytes 256 | tf_op jit(solution)/shard_map/pmax | solution.py:28
  387.4 10.9 %pmax.29 = f32[32]{0:T(128)S(1)} all-reduce(f32[32]{0:T(128)S(1)} %pmax.28), channel_id=1, replica_groups=mesh['rows_0'=4,'rows_1'=8,'rows_2'=2,'rep'=4] {'rows_1'}, use_global_device_ids=true, to_apply=%region_14.15 | all-reduce | flops 32 | bytes 256 | tf_op jit(solution)/shard_map/pmax | solution.py:28
  398.3 7.8 %pmax.30 = f32[32]{0:T(128)S(1)} all-reduce(f32[32]{0:T(128)S(1)} %pmax.29), channel_id=1, replica_groups=mesh['rows_0'=4,'rows_1'=8,'rows_2'=2,'rep'=4] {'rows_2'}, use_global_device_ids=true, to_apply=%region_15.16 | all-reduce | flops 32 | bytes 256 | tf_op jit(solution)/shard_map/pmax | solution.py:28
  406.1 9.6 %pmax.31 = f32[32]{0:T(128)} all-reduce(f32[32]{0:T(128)S(1)} %pmax.30), channel_id=1, replica_groups=mesh['rows_0'=4,'rows_1'=8,'rows_2'=2,'rep'=4] {'rep'}, use_global_device_ids=true, to_apply=%region_16.17 | all-reduce | flops 32 | bytes 256 | tf_op jit(solution)/shard_map/pmax | solution.py:28
  (40 shorter events, 2.5 us)
Async XLA Ops:
  0.6 13.6 %copy-start = (s32[1024]{0:T(1024)S(1)}, s32[1024]{0:T(1024)}, u32[]{:S(2)}) copy-start(s32[1024]{0:T(1024)} %param.14) | copy-start | bytes 12292
  3.7 10.5 %all-to-all-start = ((s32[4,1,1024]{2,1,0:T(1,128)}), s32[4,1,1024]{2,1,0:T(1,128)S(1)}, u32[]{:S(2)}, u32[]{:S(2)}) async-start(s32[4,1,1024]{2,1,0:T(1,128)} %broadcast_in_dim.104), calls=%async_computation | async-start | bytes 32768 | tf_op jit(solution)/shard_map/all_to_all | solution.py:19
  14.3 0.7 copy-start.1
where the time goes:
time: 417 us; the launch traced here: 416 us
  local copies, waits for them, and re-layouts  163 us (39%)
  blocking collectives  145 us (35%)
  other arithmetic  59.5 us (14%)
  matrix products  41.8 us (10%)
  starting transfers between devices  4.83 us (1%)
    gather x1, local copies, waits for them, and re-layouts, body(): selected = block_sums[block_of, channel, node_of, inner_of]  134 us
    all_to_all x1, blocking collectives, body(): lax.all_to_all(sectioned, ROWS, split_axis=2, concat_axis=2, tiled=True)  109 us
    eq x8, other arithmetic, add_rows(): one_hot = (piece[:, :, None] == bin_ids[None, None, :]).astype(jnp.bfloat16)  51.6 us
    dot_general x8, matrix products, add_rows(): lax.dot_general(weight_piece, one_hot, (((0,), (0,)), ((), ())), preferre...  41.8 us
    pmax x4, blocking collectives, by_axis(): shard = lax.pmax(shard, axis)  36.8 us
    unnamed x6, local copies, waits for them, and re-layouts  9.79 us
  transfers between devices with their start and end apart: 1, of which 0 were waited for; matrix products, arithmetic and copies ran while one was open for 1% of the time, Pallas kernels for 0%

commit v1 on v0

v1 whole, which is shorter than its diff:
```python
import functools

import jax
import jax.numpy as jnp
from jax import lax
from jax.experimental import pallas as pl
from jax.experimental.pallas import tpu as pltpu
from jax.sharding import Mesh
from jax.sharding import PartitionSpec as P

BINS = 128
LANES = 128
ROWS = ("rows_0", "rows_1", "rows_2")
MESH_IDS = pl.DeviceIdType.MESH
f32, bf16, i32 = jnp.float32, jnp.bfloat16, jnp.int32

l2_penalty = 1.0


def iota(shape, dim, dtype=i32):
    out = lax.broadcasted_iota(i32, shape, dim)
    if dtype == bf16:
        return out.astype(f32).astype(bf16)
    return out.astype(dtype)


def remote(src, dst, send, recv, where):
    return pltpu.make_async_remote_copy(
        src_ref=src, dst_ref=dst, send_sem=send, recv_sem=recv, device_id=where, device_id_type=MESH_IDS
    )


def kernel(ny, nz, nx, sc, split_feature, split_bin, meta, elected, binned_hbm,
           nodes_out, best_out, node_best_out,
           binned, side, side_in, outbox, zbox, ybox, acc, acc_in, top, top_z, mid, top_xy,
           load_sem, side_send, side_recv, z_send, z_recv, y_send, y_recv, core_send, core_recv,
           tz_send, tz_recv, txy_send, txy_recv):
    y, z = lax.axis_index("rows_0"), lax.axis_index("rows_1")
    core, x = lax.axis_index("rows_2"), lax.axis_index("rep")
    parent_count = split_feature.shape[0]
    node_count = elected.shape[0]
    width = binned.shape[1]
    chunks = meta.shape[1]

    load = pltpu.make_async_copy(binned_hbm, binned, load_sem)
    load.start()

    def at_x(d):
        return {"rep": lax.rem(x + d, nx)}

    def at_y(d):
        return {"rows_0": lax.rem(y + d, ny)}

    def at_z(d):
        return {"rows_1": lax.rem(z + d, nz)}

    def at_xy(dx, dy):
        return {"rep": lax.rem(x + dx, nx), "rows_0": lax.rem(y + dy, ny)}

    xy = [(dx, dy) for dx in range(nx) for dy in range(ny) if (dx, dy) != (0, 0)]
    peers = [at_z(d) for d in range(1, nz)] + [at_xy(*d) for d in xy] + [{"rows_2": 1 - core}]
    barrier = pltpu.get_barrier_semaphore()
    for peer in peers:
        pl.semaphore_signal(barrier, inc=1, device_id=peer, device_id_type=MESH_IDS)

    load.wait()
    parent_rows = iota((parent_count, LANES), 0)
    want = jnp.zeros((parent_count, width), i32)
    bound = jnp.zeros((parent_count, LANES), i32)
    for p in range(parent_count):
        want = jnp.where(iota((parent_count, width), 0) == p, split_feature[p] - x * width, want)
        bound = jnp.where(parent_rows == p, split_bin[p], bound)
    pick = jnp.where(iota((parent_count, width), 1) == want, jnp.ones((), f32), jnp.zeros((), f32)).astype(bf16)
    owned = (want[:, :LANES] >= 0) & (want[:, :LANES] < width)
    values = lax.dot_general(pick, binned[...].astype(f32).astype(bf16), (((1,), (1,)), ((), ())),
                             preferred_element_type=f32)
    bound = bound.astype(f32)
    for c in range(chunks):
        parent = meta[2, c:c + 1, :]
        hit = (parent_rows.astype(f32) == parent) & owned & (values[:, c * LANES:(c + 1) * LANES] > bound)
        side[c:c + 1, :] = jnp.max(jnp.where(hit, 1.0, 0.0), axis=0, keepdims=True)

    pl.semaphore_wait(barrier, len(peers))
    side_copies = []
    for d in range(1, nx):
        copy = remote(side, side_in.at[d - 1], side_send.at[d - 1], side_recv.at[d - 1], at_x(d))
        copy.start()
        side_copies.append(copy)
    for copy in side_copies:
        copy.wait_recv()
    went = side[...]
    for d in range(1, nx):
        went = went + side_in[d - 1]
    node = 2.0 * meta[2] + went
    nodes_out[...] = node.astype(i32)

    chosen = elected[...].astype(f32).astype(bf16)
    node_rows = iota((node_count, LANES), 0).astype(f32)
    for c in range(chunks):
        hot = jnp.where(node_rows == node[c:c + 1, :], 1.0, 0.0).astype(bf16)
        index = lax.dot_general(hot, chosen, (((0,), (0,)), ((), ())), preferred_element_type=f32).astype(i32)
        inner = index & (LANES - 1)
        picked = None
        for b in range(width // LANES):
            part = jnp.take_along_axis(binned[c * LANES:(c + 1) * LANES, b * LANES:(b + 1) * LANES], inner, axis=1)
            picked = part if b == 0 else jnp.where(index >= b * LANES, part, picked)
        turned = picked.astype(f32).T
        for yy in range(ny):
            for zz in range(nz):
                first = (yy * nz + zz) * sc
                outbox[zz, 3 + yy * sc:3 + (yy + 1) * sc, c, :] = turned[first:first + sc]
    for zz in range(nz):
        outbox[zz, 0:2] = meta[0:2]
        outbox[zz, 2] = node

    def order(i):
        half, odd = (i + 1) // 2, i % 2
        return (odd * half + (1 - odd) * (nz - half)) % nz

    for i in range(1, nz):
        d = order(i)
        remote(outbox.at[lax.rem(z + d, nz)], zbox.at[d], z_send.at[d], z_recv.at[d], at_z(d)).start()
    zbox[0] = outbox[z]

    def forwards(d):
        out = []
        for dy in range(1, ny):
            there = lax.rem(y + dy, ny)
            out.append(remote(zbox.at[d, 0:3], ybox.at[dy - 1, d, 0:3],
                              y_send.at[d, dy - 1, 0], y_recv.at[d, dy - 1], at_y(dy)))
            out.append(remote(zbox.at[d, pl.ds(3 + there * sc, sc)], ybox.at[dy - 1, d, 3:3 + sc],
                              y_send.at[d, dy - 1, 1], y_recv.at[d, dy - 1], at_y(dy)))
        return out

    def add(box, d, shift):
        bin_rows = iota((BINS, LANES), 0, bf16)
        node_of = iota((node_count, LANES), 0, bf16)
        one, zero = jnp.ones((), bf16), jnp.zeros((), bf16)
        grads, hesses = [], []
        for c in range(chunks):
            here = node_of == box[d, 2, c:c + 1, :].astype(bf16)
            grads.append(jnp.where(here, box[d, 0, c:c + 1, :].astype(bf16), zero))
            hesses.append(jnp.where(here, box[d, 1, c:c + 1, :].astype(bf16), zero))
        weights = jnp.concatenate([jnp.concatenate(grads, axis=1), jnp.concatenate(hesses, axis=1)], axis=0)
        hots = []
        for s in range(sc):
            row = [box[d, shift + s, c:c + 1, :].astype(bf16) for c in range(chunks)]
            hots.append(jnp.concatenate([jnp.where(bin_rows == r, one, zero) for r in row], axis=1))
        acc[...] += lax.dot_general(weights, jnp.concatenate(hots, axis=0), (((1,), (1,)), ((), ())),
                                    preferred_element_type=f32)

    def add_all(d):
        add(zbox, d, 3 + y * sc)

        def one(dy, carry):
            pltpu.make_async_copy(ybox.at[dy, d], ybox.at[dy, d], y_recv.at[d, dy]).wait()
            add(ybox.at[dy], d, 3)
            return carry

        lax.fori_loop(0, ny - 1, one, 0)

    acc[...] = jnp.zeros_like(acc)
    for copy in forwards(0):
        copy.start()

    def step(i, carry):
        d = order(i)
        pltpu.make_async_copy(zbox.at[d], zbox.at[d], z_recv.at[d]).wait()
        for copy in forwards(d):
            copy.start()
        add_all(order(i - 1))
        return carry

    lax.fori_loop(1, nz, step, 0)
    add_all(order(nz - 1))

    swap = remote(acc, acc_in, core_send, core_recv, {"rows_2": 1 - core})
    swap.start()
    swap.wait_recv()
    hist = acc[...] + acc_in[...]
    upto = jnp.where(iota((BINS, BINS), 0) <= iota((BINS, BINS), 1), 1.0, 0.0)
    lane = iota((node_count, BINS), 1)
    low = jnp.full((), -3.0e38, f32)
    best = []
    for s in range(sc):
        left = jnp.dot(hist[:, s * BINS:(s + 1) * BINS], upto, precision=lax.Precision.HIGHEST,
                       preferred_element_type=f32)
        left_grad, left_hess = left[:node_count], left[node_count:]
        total_grad, total_hess = left_grad[:, BINS - 1:], left_hess[:, BINS - 1:]
        gain = 0.5 * (left_grad * left_grad / (left_hess + l2_penalty)
                      + (total_grad - left_grad) ** 2 / (total_hess - left_hess + l2_penalty)
                      - total_grad * total_grad / (total_hess + l2_penalty))
        best.append(jnp.max(jnp.where(lane < BINS - 1, gain, low), axis=1, keepdims=True))
    half = sc // 2
    for s in range(half):
        best_out[:, s:s + 1] = jnp.where(core == 0, best[s], best[half + s])
    column = functools.reduce(jnp.maximum, best)
    diagonal = iota((node_count, LANES), 0) == iota((node_count, LANES), 1)
    top[...] = jnp.max(jnp.where(diagonal, column, low), axis=0, keepdims=True)

    copies = []
    for d in range(1, nz):
        copy = remote(top, top_z.at[d - 1], tz_send.at[d - 1], tz_recv.at[d - 1], at_z(d))
        copy.start()
        copies.append(copy)
    for copy in copies:
        copy.wait_recv()
    highest = top[...]
    for d in range(1, nz):
        highest = jnp.maximum(highest, top_z[d - 1])
    mid[...] = highest
    for i, (dx, dy) in enumerate(xy):
        copy = remote(mid, top_xy.at[i], txy_send.at[i], txy_recv.at[i], at_xy(dx, dy))
        copy.start()
        copies.append(copy)
    for copy in copies[nz - 1:]:
        copy.wait_recv()
    for i in range(len(xy)):
        highest = jnp.maximum(highest, top_xy[i])
    node_best_out[...] = highest[:, :node_count]

    for copy in copies + side_copies + [swap]:
        copy.wait_send()
    for d in range(1, nz):
        remote(outbox.at[0], zbox.at[d], z_send.at[d], z_recv.at[d], at_z(d)).wait_send()
    for d in range(nz):
        for copy in forwards(d):
            copy.wait_send()


def body(sizes, binned, gradients, hessians, parents, split_feature, split_bin, elected):
    ny, nz, nx = sizes
    rows_here, width = binned.shape
    node_count, slots_here = elected.shape
    chunks = rows_here // LANES
    sc = slots_here // (ny * nz)
    meta = jnp.stack([gradients.astype(f32), hessians.astype(f32), parents.astype(f32)]).reshape(3, chunks, LANES)
    vmem, smem = pl.BlockSpec(memory_space=pltpu.VMEM), pl.BlockSpec(memory_space=pltpu.SMEM)
    dma = pltpu.SemaphoreType.DMA
    nodes, best, node_best = pl.pallas_call(
        functools.partial(kernel, ny, nz, nx, sc),
        out_shape=(
            jax.ShapeDtypeStruct((chunks, LANES), i32),
            jax.ShapeDtypeStruct((node_count, sc // 2), f32),
            jax.ShapeDtypeStruct((1, node_count), f32),
        ),
        in_specs=[smem, smem, vmem, vmem, pl.BlockSpec(memory_space=pl.ANY)],
        out_specs=(vmem, vmem, vmem),
        scratch_shapes=[
            pltpu.VMEM((rows_here, width), i32),
            pltpu.VMEM((chunks, LANES), f32),
            pltpu.VMEM((nx - 1, chunks, LANES), f32),
            pltpu.VMEM((nz, 3 + ny * sc, chunks, LANES), f32),
            pltpu.VMEM((nz, 3 + ny * sc, chunks, LANES), f32),
            pltpu.VMEM((ny - 1, nz, 3 + sc, chunks, LANES), f32),
            pltpu.VMEM((2 * node_count, sc * BINS), f32),
            pltpu.VMEM((2 * node_count, sc * BINS), f32),
            pltpu.VMEM((1, LANES), f32),
            pltpu.VMEM((nz - 1, 1, LANES), f32),
            pltpu.VMEM((1, LANES), f32),
            pltpu.VMEM((nx * ny - 1, 1, LANES), f32),
            dma,
            dma((nx - 1,)), dma((nx - 1,)),
            dma((nz,)), dma((nz,)),
            dma((nz, ny - 1, 2)), dma((nz, ny - 1)),
            dma, dma,
            dma((nz - 1,)), dma((nz - 1,)),
            dma((nx * ny - 1,)), dma((nx * ny - 1,)),
        ],
        compiler_params=pltpu.CompilerParams(collective_id=0, has_side_effects=True),
        name="level",
    )(split_feature, split_bin, meta, elected, binned)
    return nodes.reshape(rows_here), best[:, None, :], node_best.reshape(node_count)


def solution(mesh):
    ny, nz, nx = 4, 8, mesh.shape["rep"]
    finer = Mesh(mesh.devices.reshape(ny, nz, 2, nx), ("rows_0", "rows_1", "rows_2", "rep"))
    placed = (P(ROWS, "rep"), P(ROWS), P(ROWS), P(ROWS), P(), P(), P(None, "rep"))
    return jax.shard_map(
        functools.partial(body, (ny, nz, nx)),
        mesh=finer,
        in_specs=placed,
        out_specs=(P(ROWS), P(None, "rep", ROWS), P()),
        check_vma=False,
    )
```

time: 417 us -> 57.8 us (0.14)
  local copies, waits for them, and re-layouts: 163 us -> 2.54 us
  blocking collectives: 145 us -> 0 us
  other arithmetic: 59.5 us -> 1.31 us
  Pallas kernels: 0 us -> 53 us
  matrix products: 41.8 us -> 0 us
  starting transfers between devices: 4.83 us -> 0 us
    gather x1 -> x0, local copies, waits for them, and re-layouts: 134 us -> none  [body(): selected = block_sums[block_of, channel, node_of, inner_of]]
    all_to_all x1 -> x0, blocking collectives: 109 us -> none  [body(): lax.all_to_all(sectioned, ROWS, split_axis=2, concat_axis=2, tiled=True)]
    pallas_call x0 -> x1, Pallas kernels: none -> 53 us  [body(): pl.pallas_call(functools.partial(kernel, ny, nz, nx, sc), out_shape=(jax....]
    eq x8 -> x0, other arithmetic: 51.6 us -> none  [add_rows(): one_hot = (piece[:, :, None] == bin_ids[None, None, :]).astype(jnp.bfloat16)]
    dot_general x8 -> x0, matrix products: 41.8 us -> none  [add_rows(): lax.dot_general(weight_piece, one_hot, (((0,), (0,)), ((), ())), preferre...]
    pmax x4 -> x0, blocking collectives: 36.8 us -> none  [by_axis(): shard = lax.pmax(shard, axis)]
    unnamed x6 -> x10, local copies, waits for them, and re-layouts: 9.79 us -> 1.19 us
    reshape x2 -> x0, local copies, waits for them, and re-layouts: 6.51 us -> none  [the longest x1 4.57 us: body(): sectioned = selected.reshape(2, node_count, row_devices, owned_slots, BINS)]
  transfers between devices with their start and end apart: 1 -> 0, of which waited for: 0 -> 0; matrix products, arithmetic and copies ran while one was open for 1% -> 0% of each run, Pallas kernels for 0% -> 0%
where the time goes in v1:
time: 57.8 us; the launch traced here: 57.5 us
  Pallas kernels  53 us (92%)
  local copies, waits for them, and re-layouts  2.54 us (4%)
  other arithmetic  1.31 us (2%)
  between operations  0.67 us (1%)
    pallas_call x1, Pallas kernels, body(): pl.pallas_call(functools.partial(kernel, ny, nz, nx, sc), out_shape=(jax....  53 us
    pallas_call x1, local copies, waits for them, and re-layouts, body(): pl.pallas_call(functools.partial(kernel, ny, nz, nx, sc), out_shape=(jax....  1.35 us
    another operation x3, other arithmetic, body(): jnp.stack([gradients.astype(f32), hessians.astype(f32), parents.astype(f3...  1.31 us
    unnamed x10, local copies, waits for them, and re-layouts  1.19 us

profile of v1, /device:TPU:1, one launch (start us, length us, event | category | flops | bytes accessed | tf_op | source)
XLA Modules:
  0.0 57.5 jit_solution(7248739358914145694)
XLA Ops:
  0.6 0.0 copy-start.1
  0.6 0.0 copy-start.2
  0.7 0.7 %convert_bitcast_fusion = f32[1,8,128]{2,1,0:T(8,128)S(1)} fusion(s32[1024]{0:T(1024)} %param.10), kind=kLoop, calls=%fused_computation.1 | loop fusion | flops 1024 | bytes 8192 | tf_op jit(solution)/shard_map/stack | solution.py:237
  1.4 0.0 copy-done.1
  1.4 0.0 copy-done.2
  1.4 0.6 %pad_maximum_fusion.meta = f32[3,8,128]{2,1,0:T(8,128)} fusion(f32[1,8,128]{2,1,0:T(8,128)S(1)} %convert_bitcast_fusion, f32[1,8,128]{2,1,0:T(8,128)S(1)} %get-tuple-element.9, f32[1,8,128]{2,1,0:T(8,128)S(1)} %get-tuple-element.10), kind=kLoop, calls=%fused_computation | loop fusion | flops 6144 | bytes 24576 | tf_op jit(solution)/shard_map/stack | solution.py:237
  2.0 53.0 %level.1 = (s32[8,128]{1,0:T(8,128)}, f32[32,2]{1,0:T(8,128)}, f32[1,32]{1,0:T(1,128)}) custom-call(s32[16]{0:T(128)} %split_feature.1, s32[16]{0:T(128)} %split_bin.1, f32[3,8,128]{2,1,0:T(8,128)} %pad_maximum_fusion.meta, s32[32,128]{1,0:T(8,128)} %elected.1, s32[1024,256]{1,0:T(8,128)} %binned_hbm.1), custom_call_target="tpu_custom_call" | custom-call | tf_op jit(solution)/shard_map/level/pallas_call | solution.py:240
  54.9 0.0 copy-start
  54.9 1.4 %copy.10 = f32[32,2]{0,1:T(2,128)} copy(f32[32,2]{1,0:T(8,128)} %get-tuple-element.7) | data formatting | bytes 512 | tf_op jit(solution)/shard_map/level/pallas_call | solution.py:240
  56.3 0.0 copy-done
  56.3 0.0 copy-start.3
  56.3 0.6 %copy.13 = s32[1024]{0:T(1024)} copy(s32[1024]{0:T(1024)S(1)} %bitcast.11) | data formatting | bytes 8192
  56.9 0.1 copy-done.3
  57.0 0.5 copy.14
  (1 shorter events, 0.0 us)
Async XLA Ops:
  0.6 0.7 %copy-start.1 = (bf16[1024]{0:T(1024)(128)(2,1)S(1)}, bf16[1024]{0:T(1024)(128)(2,1)}, u32[]{:S(2)}) copy-start(bf16[1024]{0:T(1024)(128)(2,1)} %param.9) | copy-start | bytes 6148
  0.6 0.7 %copy-start.2 = (bf16[1024]{0:T(1024)(128)(2,1)S(1)}, bf16[1024]{0:T(1024)(128)(2,1)}, u32[]{:S(2)}) copy-start(bf16[1024]{0:T(1024)(128)(2,1)} %param.8) | copy-start | bytes 6148
  54.9 1.4 %copy-start = (s32[8,128]{1,0:T(8,128)S(1)}, s32[8,128]{1,0:T(8,128)}, u32[]{:S(2)}) copy-start(s32[8,128]{1,0:T(8,128)} %get-tuple-element.6) | copy-start | bytes 12292
  56.3 0.7 %copy-start.3 = (f32[1,32]{1,0:T(1,128)S(1)}, f32[1,32]{1,0:T(1,128)}, u32[]{:S(2)}) copy-start(f32[1,32]{1,0:T(1,128)} %get-tuple-element.8) | copy-start | bytes 388

commit v2 on v1

--- a/solution.py
+++ b/solution.py
@@ -32,9 +32,10 @@
 
 def kernel(ny, nz, nx, sc, split_feature, split_bin, meta, elected, binned_hbm,
            nodes_out, best_out, node_best_out,
-           binned, side, side_in, outbox, zbox, ybox, acc, acc_in, top, top_z, mid, top_xy,
-           load_sem, side_send, side_recv, z_send, z_recv, y_send, y_recv, core_send, core_recv,
-           tz_send, tz_recv, txy_send, txy_recv):
+           binned, side, side_in, outbox, zbox, node_box, stats_box, weights, acc, acc_y, mine, acc_in,
+           top, top_z, mid, top_xy,
+           load_sem, side_send, side_recv, z_send, z_recv, node_send, node_recv, stats_send, stats_recv,
+           y_send, y_recv, core_send, core_recv, tz_send, tz_recv, txy_send, txy_recv):
     y, z = lax.axis_index("rows_0"), lax.axis_index("rows_1")
     core, x = lax.axis_index("rows_2"), lax.axis_index("rep")
     parent_count = split_feature.shape[0]
@@ -56,6 +57,10 @@
 
     def at_xy(dx, dy):
         return {"rep": lax.rem(x + dx, nx), "rows_0": lax.rem(y + dy, ny)}
+
+    def order(i):
+        half, odd = (i + 1) // 2, i % 2
+        return (odd * half + (1 - odd) * (nz - half)) % nz
 
     xy = [(dx, dy) for dx in range(nx) for dy in range(ny) if (dx, dy) != (0, 0)]
     peers = [at_z(d) for d in range(1, nz)] + [at_xy(*d) for d in xy] + [{"rows_2": 1 - core}]
@@ -86,6 +91,10 @@
         copy = remote(side, side_in.at[d - 1], side_send.at[d - 1], side_recv.at[d - 1], at_x(d))
         copy.start()
         side_copies.append(copy)
+    stats = meta.at[0:2]
+    for i in range(1, nz):
+        d = order(i)
+        remote(stats, stats_box.at[d], stats_send.at[d], stats_recv.at[d], at_z(d)).start()
     for copy in side_copies:
         copy.wait_recv()
     went = side[...]
@@ -96,6 +105,7 @@
 
     chosen = elected[...].astype(f32).astype(bf16)
     node_rows = iota((node_count, LANES), 0).astype(f32)
+    node_box[0] = node
     for c in range(chunks):
         hot = jnp.where(node_rows == node[c:c + 1, :], 1.0, 0.0).astype(bf16)
         index = lax.dot_general(hot, chosen, (((0,), (0,)), ((), ())), preferred_element_type=f32).astype(i32)
@@ -108,76 +118,92 @@
         for yy in range(ny):
             for zz in range(nz):
                 first = (yy * nz + zz) * sc
-                outbox[zz, 3 + yy * sc:3 + (yy + 1) * sc, c, :] = turned[first:first + sc]
-    for zz in range(nz):
-        outbox[zz, 0:2] = meta[0:2]
-        outbox[zz, 2] = node
-
-    def order(i):
-        half, odd = (i + 1) // 2, i % 2
-        return (odd * half + (1 - odd) * (nz - half)) % nz
-
-    for i in range(1, nz):
-        d = order(i)
-        remote(outbox.at[lax.rem(z + d, nz)], zbox.at[d], z_send.at[d], z_recv.at[d], at_z(d)).start()
-    zbox[0] = outbox[z]
-
-    def forwards(d):
-        out = []
-        for dy in range(1, ny):
-            there = lax.rem(y + dy, ny)
-            out.append(remote(zbox.at[d, 0:3], ybox.at[dy - 1, d, 0:3],
-                              y_send.at[d, dy - 1, 0], y_recv.at[d, dy - 1], at_y(dy)))
-            out.append(remote(zbox.at[d, pl.ds(3 + there * sc, sc)], ybox.at[dy - 1, d, 3:3 + sc],
-                              y_send.at[d, dy - 1, 1], y_recv.at[d, dy - 1], at_y(dy)))
-        return out
-
-    def add(box, d, shift):
+                outbox[zz, yy, :, c, :] = turned[first:first + sc]
+        if c == 1:
+            for i in range(1, nz):
+                d = order(i)
+                remote(node_box.at[0], node_box.at[d], node_send.at[d], node_recv.at[d], at_z(d)).start()
+
+    def bins_to(j, d):
+        there = lax.rem(y + 1 + j, ny)
+        return remote(outbox.at[lax.rem(z + d, nz), there], zbox.at[j, d], z_send.at[j, d], z_recv.at[j, d], at_z(d))
+
+    for j in range(ny):
+        for i in range(1, nz):
+            bins_to(j, order(i)).start()
+
+    def weigh(d):
+        node_of = iota((node_count, LANES), 0, bf16)
+        zero = jnp.zeros((), bf16)
+        for c in range(chunks):
+            here = node_of == node_box[d, c:c + 1, :].astype(bf16)
+            at = slice(c * LANES, (c + 1) * LANES)
+            weights[d, :node_count, at] = jnp.where(here, stats_box[d, 0, c:c + 1, :].astype(bf16), zero)
+            weights[d, node_count:, at] = jnp.where(here, stats_box[d, 1, c:c + 1, :].astype(bf16), zero)
+
+    def counted(box, d):
         bin_rows = iota((BINS, LANES), 0, bf16)
-        node_of = iota((node_count, LANES), 0, bf16)
         one, zero = jnp.ones((), bf16), jnp.zeros((), bf16)
-        grads, hesses = [], []
-        for c in range(chunks):
-            here = node_of == box[d, 2, c:c + 1, :].astype(bf16)
-            grads.append(jnp.where(here, box[d, 0, c:c + 1, :].astype(bf16), zero))
-            hesses.append(jnp.where(here, box[d, 1, c:c + 1, :].astype(bf16), zero))
-        weights = jnp.concatenate([jnp.concatenate(grads, axis=1), jnp.concatenate(hesses, axis=1)], axis=0)
         hots = []
         for s in range(sc):
-            row = [box[d, shift + s, c:c + 1, :].astype(bf16) for c in range(chunks)]
+            row = [box[s, c:c + 1, :].astype(bf16) for c in range(chunks)]
             hots.append(jnp.concatenate([jnp.where(bin_rows == r, one, zero) for r in row], axis=1))
-        acc[...] += lax.dot_general(weights, jnp.concatenate(hots, axis=0), (((1,), (1,)), ((), ())),
-                                    preferred_element_type=f32)
-
-    def add_all(d):
-        add(zbox, d, 3 + y * sc)
-
-        def one(dy, carry):
-            pltpu.make_async_copy(ybox.at[dy, d], ybox.at[dy, d], y_recv.at[d, dy]).wait()
-            add(ybox.at[dy], d, 3)
-            return carry
-
-        lax.fori_loop(0, ny - 1, one, 0)
-
-    acc[...] = jnp.zeros_like(acc)
-    for copy in forwards(0):
-        copy.start()
-
-    def step(i, carry):
+        return lax.dot_general(weights[d], jnp.concatenate(hots, axis=0), (((1,), (1,)), ((), ())),
+                               preferred_element_type=f32)
+
+    def wait_for(ref, sem):
+        pltpu.make_async_copy(ref, ref, sem).wait()
+
+    stats_box[0] = meta[0:2]
+    weigh(0)
+
+    def own(j, carry):
+        acc[j] = counted(outbox.at[z, lax.rem(y + 1 + j, ny)], 0)
+        return carry
+
+    lax.fori_loop(0, ny, own, 0)
+
+    def weigh_next(i, carry):
         d = order(i)
-        pltpu.make_async_copy(zbox.at[d], zbox.at[d], z_recv.at[d]).wait()
-        for copy in forwards(d):
-            copy.start()
-        add_all(order(i - 1))
+        wait_for(stats_box.at[d], stats_recv.at[d])
+        wait_for(node_box.at[d], node_recv.at[d])
+        weigh(d)
         return carry
 
-    lax.fori_loop(1, nz, step, 0)
-    add_all(order(nz - 1))
-
-    swap = remote(acc, acc_in, core_send, core_recv, {"rows_2": 1 - core})
+    lax.fori_loop(1, nz, weigh_next, 0)
+
+    def to_owner(j):
+        return remote(acc.at[j], acc_y.at[j], y_send.at[j], y_recv.at[j], at_y(1 + j))
+
+    def add_group(j, group):
+        for d in group:
+            wait_for(zbox.at[j, d], z_recv.at[j, d])
+        acc[j] += functools.reduce(jnp.add, [counted(zbox.at[j, d], d) for d in group])
+
+    groups = [[order(i) for i in range(1, nz)][k:k + 4] for k in range(0, nz - 1, 4)]
+
+    def next_round(j, carry):
+        add_group(j, groups[0])
+
+        @pl.when(j > 0)
+        def _():
+            to_owner(j - 1).start()
+
+        for group in groups[1:]:
+            add_group(j, group)
+        return carry
+
+    lax.fori_loop(0, ny, next_round, 0)
+    total = acc[ny - 1]
+    for j in range(ny - 1):
+        to_owner(j).wait_recv()
+        total = total + acc_y[j]
+    mine[...] = total
+
+    swap = remote(mine, acc_in, core_send, core_recv, {"rows_2": 1 - core})
     swap.start()
     swap.wait_recv()
-    hist = acc[...] + acc_in[...]
+    hist = total + acc_in[...]
     upto = jnp.where(iota((BINS, BINS), 0) <= iota((BINS, BINS), 1), 1.0, 0.0)
     lane = iota((node_count, BINS), 1)
     low = jnp.full((), -3.0e38, f32)
@@ -222,10 +248,12 @@
     for copy in copies + side_copies + [swap]:
         copy.wait_send()
     for d in range(1, nz):
-        remote(outbox.at[0], zbox.at[d], z_send.at[d], z_recv.at[d], at_z(d)).wait_send()
-    for d in range(nz):
-        for copy in forwards(d):
-            copy.wait_send()
+        remote(stats, stats_box.at[d], stats_send.at[d], stats_recv.at[d], at_z(d)).wait_send()
+        remote(node_box.at[0], node_box.at[d], node_send.at[d], node_recv.at[d], at_z(d)).wait_send()
+        for j in range(ny):
+            bins_to(j, d).wait_send()
+    for j in range(ny - 1):
+        to_owner(j).wait_send()
 
 
 def body(sizes, binned, gradients, hessians, parents, split_feature, split_bin, elected):
@@ -250,9 +278,13 @@
             pltpu.VMEM((rows_here, width), i32),
             pltpu.VMEM((chunks, LANES), f32),
             pltpu.VMEM((nx - 1, chunks, LANES), f32),
-            pltpu.VMEM((nz, 3 + ny * sc, chunks, LANES), f32),
-            pltpu.VMEM((nz, 3 + ny * sc, chunks, LANES), f32),
-            pltpu.VMEM((ny - 1, nz, 3 + sc, chunks, LANES), f32),
+            pltpu.VMEM((nz, ny, sc, chunks, LANES), f32),
+            pltpu.VMEM((ny, nz, sc, chunks, LANES), f32),
+            pltpu.VMEM((nz, chunks, LANES), f32),
+            pltpu.VMEM((nz, 2, chunks, LANES), f32),
+            pltpu.VMEM((nz, 2 * node_count, rows_here), bf16),
+            pltpu.VMEM((ny, 2 * node_count, sc * BINS), f32),
+            pltpu.VMEM((ny - 1, 2 * node_count, sc * BINS), f32),
             pltpu.VMEM((2 * node_count, sc * BINS), f32),
             pltpu.VMEM((2 * node_count, sc * BINS), f32),
             pltpu.VMEM((1, LANES), f32),
@@ -261,8 +293,10 @@
             pltpu.VMEM((nx * ny - 1, 1, LANES), f32),
             dma,
             dma((nx - 1,)), dma((nx - 1,)),
+            dma((ny, nz)), dma((ny, nz)),
             dma((nz,)), dma((nz,)),
-            dma((nz, ny - 1, 2)), dma((nz, ny - 1)),
+            dma((nz,)), dma((nz,)),
+            dma((ny - 1,)), dma((ny - 1,)),
             dma, dma,
             dma((nz - 1,)), dma((nz - 1,)),
             dma((nx * ny - 1,)), dma((nx * ny - 1,)),

time: 57.8 us -> 51.1 us (0.88)
  Pallas kernels: 53 us -> 46.3 us
    pallas_call x1, Pallas kernels: 53 us -> 46.3 us  [body(): pl.pallas_call(functools.partial(kernel, ny, nz, nx, sc), out_shape=(jax....]
where the time goes in v2:
time: 51.1 us; the launch traced here: 50.8 us
  Pallas kernels  46.3 us (91%)
  local copies, waits for them, and re-layouts  2.54 us (5%)
  other arithmetic  1.31 us (3%)
  between operations  0.67 us (1%)
    pallas_call x1, Pallas kernels, body(): pl.pallas_call(functools.partial(kernel, ny, nz, nx, sc), out_shape=(jax....  46.3 us
    pallas_call x1, local copies, waits for them, and re-layouts, body(): pl.pallas_call(functools.partial(kernel, ny, nz, nx, sc), out_shape=(jax....  1.35 us
    another operation x3, other arithmetic, body(): jnp.stack([gradients.astype(f32), hessians.astype(f32), parents.astype(f3...  1.31 us
    unnamed x10, local copies, waits for them, and re-layouts  1.19 us

profile of v2, /device:TPU:1, one launch (start us, length us, event | category | flops | bytes accessed | tf_op | source)
XLA Modules:
  0.0 50.8 jit_solution(12742092745401419131)
XLA Ops:
  0.6 0.0 copy-start.1
  0.6 0.0 copy-start.2
  0.7 0.7 %convert_bitcast_fusion = f32[1,8,128]{2,1,0:T(8,128)S(1)} fusion(s32[1024]{0:T(1024)} %param.10), kind=kLoop, calls=%fused_computation.1 | loop fusion | flops 1024 | bytes 8192 | tf_op jit(solution)/shard_map/stack | solution.py:265
  1.4 0.0 copy-done.1
  1.4 0.0 copy-done.2
  1.4 0.6 %pad_maximum_fusion.meta = f32[3,8,128]{2,1,0:T(8,128)} fusion(f32[1,8,128]{2,1,0:T(8,128)S(1)} %convert_bitcast_fusion, f32[1,8,128]{2,1,0:T(8,128)S(1)} %get-tuple-element.9, f32[1,8,128]{2,1,0:T(8,128)S(1)} %get-tuple-element.10), kind=kLoop, calls=%fused_computation | loop fusion | flops 6144 | bytes 24576 | tf_op jit(solution)/shard_map/stack | solution.py:265
  2.0 46.3 %level.1 = (s32[8,128]{1,0:T(8,128)}, f32[32,2]{1,0:T(8,128)}, f32[1,32]{1,0:T(1,128)}) custom-call(s32[16]{0:T(128)} %split_feature.1, s32[16]{0:T(128)} %split_bin.1, f32[3,8,128]{2,1,0:T(8,128)} %pad_maximum_fusion.meta, s32[32,128]{1,0:T(8,128)} %elected.1, s32[1024,256]{1,0:T(8,128)} %binned_hbm.1), custom_call_target="tpu_custom_call" | custom-call | tf_op jit(solution)/shard_map/level/pallas_call | solution.py:268
  48.3 0.0 copy-start
  48.3 1.4 %copy.10 = f32[32,2]{0,1:T(2,128)} copy(f32[32,2]{1,0:T(8,128)} %get-tuple-element.7) | data formatting | bytes 512 | tf_op jit(solution)/shard_map/level/pallas_call | solution.py:268
  49.7 0.0 copy-done
  49.7 0.0 copy-start.3
  49.7 0.6 %copy.13 = s32[1024]{0:T(1024)} copy(s32[1024]{0:T(1024)S(1)} %bitcast.11) | data formatting | bytes 8192
  50.3 0.1 copy-done.3
  50.3 0.5 %copy.14 = f32[32]{0:T(128)} copy(f32[32]{0:T(128)S(1)} %bitcast.13) | data formatting | bytes 256
  (1 shorter events, 0.0 us)
Async XLA Ops:
  0.6 0.7 %copy-start.1 = (bf16[1024]{0:T(1024)(128)(2,1)S(1)}, bf16[1024]{0:T(1024)(128)(2,1)}, u32[]{:S(2)}) copy-start(bf16[1024]{0:T(1024)(128)(2,1)} %param.9) | copy-start | bytes 6148
  0.6 0.7 %copy-start.2 = (bf16[1024]{0:T(1024)(128)(2,1)S(1)}, bf16[1024]{0:T(1024)(128)(2,1)}, u32[]{:S(2)}) copy-start(bf16[1024]{0:T(1024)(128)(2,1)} %param.8) | copy-start | bytes 6148
  48.3 1.4 %copy-start = (s32[8,128]{1,0:T(8,128)S(1)}, s32[8,128]{1,0:T(8,128)}, u32[]{:S(2)}) copy-start(s32[8,128]{1,0:T(8,128)} %get-tuple-element.6) | copy-start | bytes 12292
  49.7 0.7 %copy-start.3 = (f32[1,32]{1,0:T(1,128)S(1)}, f32[1,32]{1,0:T(1,128)}, u32[]{:S(2)}) copy-start(f32[1,32]{1,0:T(1,128)} %get-tuple-element.8) | copy-start | bytes 388

commit v3 on v2

--- a/solution.py
+++ b/solution.py
@@ -12,7 +12,7 @@
 LANES = 128
 ROWS = ("rows_0", "rows_1", "rows_2")
 MESH_IDS = pl.DeviceIdType.MESH
-f32, bf16, i32 = jnp.float32, jnp.bfloat16, jnp.int32
+f32, bf16, i32, f8 = jnp.float32, jnp.bfloat16, jnp.int32, jnp.float8_e4m3fn
 
 l2_penalty = 1.0
 
@@ -30,18 +30,18 @@
     )
 
 
-def kernel(ny, nz, nx, sc, split_feature, split_bin, meta, elected, binned_hbm,
+def kernel(ny, nz, nx, sc, split_feature, split_bin, gradients, hessians, parents, elected, binned_hbm,
            nodes_out, best_out, node_best_out,
-           binned, side, side_in, outbox, zbox, node_box, stats_box, weights, acc, acc_y, mine, acc_in,
-           top, top_z, mid, top_xy,
+           binned, side, side_in, left_box, outbox, zbox, node_box, stats_box, weights, acc, acc_y, mine, acc_in,
+           top, tops,
            load_sem, side_send, side_recv, z_send, z_recv, node_send, node_recv, stats_send, stats_recv,
-           y_send, y_recv, core_send, core_recv, tz_send, tz_recv, txy_send, txy_recv):
+           y_send, y_recv, core_send, core_recv, top_send, top_recv):
     y, z = lax.axis_index("rows_0"), lax.axis_index("rows_1")
     core, x = lax.axis_index("rows_2"), lax.axis_index("rep")
     parent_count = split_feature.shape[0]
     node_count = elected.shape[0]
     width = binned.shape[1]
-    chunks = meta.shape[1]
+    chunks = parents.shape[0]
 
     load = pltpu.make_async_copy(binned_hbm, binned, load_sem)
     load.start()
@@ -67,6 +67,10 @@
     barrier = pltpu.get_barrier_semaphore()
     for peer in peers:
         pl.semaphore_signal(barrier, inc=1, device_id=peer, device_id_type=MESH_IDS)
+
+    stats_box[0, 0] = gradients[...].astype(f32)
+    stats_box[0, 1] = hessians[...].astype(f32)
+    parent = parents[...].astype(f32)
 
     load.wait()
     parent_rows = iota((parent_count, LANES), 0)
@@ -81,8 +85,7 @@
                              preferred_element_type=f32)
     bound = bound.astype(f32)
     for c in range(chunks):
-        parent = meta[2, c:c + 1, :]
-        hit = (parent_rows.astype(f32) == parent) & owned & (values[:, c * LANES:(c + 1) * LANES] > bound)
+        hit = (parent_rows.astype(f32) == parent[c:c + 1]) & owned & (values[:, c * LANES:(c + 1) * LANES] > bound)
         side[c:c + 1, :] = jnp.max(jnp.where(hit, 1.0, 0.0), axis=0, keepdims=True)
 
     pl.semaphore_wait(barrier, len(peers))
@@ -91,38 +94,43 @@
         copy = remote(side, side_in.at[d - 1], side_send.at[d - 1], side_recv.at[d - 1], at_x(d))
         copy.start()
         side_copies.append(copy)
-    stats = meta.at[0:2]
+    stats = stats_box.at[0]
     for i in range(1, nz):
         d = order(i)
         remote(stats, stats_box.at[d], stats_send.at[d], stats_recv.at[d], at_z(d)).start()
+    chosen = elected[...].astype(f32).astype(bf16)
+    node_rows = iota((node_count, LANES), 0).astype(f32)
+    for c in range(chunks):
+        rows = slice(c * LANES, (c + 1) * LANES)
+        packed = binned[rows, :LANES]
+        for b in range(1, width // LANES):
+            packed = packed + (binned[rows, b * LANES:(b + 1) * LANES] << (8 * b))
+        for way, box in ((0, left_box), (1, outbox)):
+            hot = jnp.where(node_rows == 2.0 * parent[c:c + 1] + way, 1.0, 0.0).astype(bf16)
+            index = lax.dot_general(hot, chosen, (((0,), (0,)), ((), ())), preferred_element_type=f32).astype(i32)
+            found = jnp.take_along_axis(packed, index & (LANES - 1), axis=1, mode="promise_in_bounds")
+            found = (found >> ((index >> 7) << 3)) & (BINS - 1)
+            turned = found.astype(f32).T
+            for yy in range(ny):
+                for zz in range(nz):
+                    first = (yy * nz + zz) * sc
+                    box[zz, yy, :, c, :] = turned[first:first + sc]
+
     for copy in side_copies:
         copy.wait_recv()
     went = side[...]
     for d in range(1, nx):
         went = went + side_in[d - 1]
-    node = 2.0 * meta[2] + went
+    node = 2.0 * parent + went
     nodes_out[...] = node.astype(i32)
-
-    chosen = elected[...].astype(f32).astype(bf16)
-    node_rows = iota((node_count, LANES), 0).astype(f32)
     node_box[0] = node
-    for c in range(chunks):
-        hot = jnp.where(node_rows == node[c:c + 1, :], 1.0, 0.0).astype(bf16)
-        index = lax.dot_general(hot, chosen, (((0,), (0,)), ((), ())), preferred_element_type=f32).astype(i32)
-        inner = index & (LANES - 1)
-        picked = None
-        for b in range(width // LANES):
-            part = jnp.take_along_axis(binned[c * LANES:(c + 1) * LANES, b * LANES:(b + 1) * LANES], inner, axis=1)
-            picked = part if b == 0 else jnp.where(index >= b * LANES, part, picked)
-        turned = picked.astype(f32).T
-        for yy in range(ny):
-            for zz in range(nz):
-                first = (yy * nz + zz) * sc
-                outbox[zz, yy, :, c, :] = turned[first:first + sc]
-        if c == 1:
-            for i in range(1, nz):
-                d = order(i)
-                remote(node_box.at[0], node_box.at[d], node_send.at[d], node_recv.at[d], at_z(d)).start()
+    right = (went > 0.0)[None]
+    for yy in range(ny):
+        for zz in range(nz):
+            outbox[zz, yy] = jnp.where(right, outbox[zz, yy], left_box[zz, yy])
+    for i in range(1, nz):
+        d = order(i)
+        remote(node_box.at[0], node_box.at[d], node_send.at[d], node_recv.at[d], at_z(d)).start()
 
     def bins_to(j, d):
         there = lax.rem(y + 1 + j, ny)
@@ -148,13 +156,12 @@
         for s in range(sc):
             row = [box[s, c:c + 1, :].astype(bf16) for c in range(chunks)]
             hots.append(jnp.concatenate([jnp.where(bin_rows == r, one, zero) for r in row], axis=1))
-        return lax.dot_general(weights[d], jnp.concatenate(hots, axis=0), (((1,), (1,)), ((), ())),
+        return lax.dot_general(weights[d], jnp.concatenate(hots, axis=0).astype(f8), (((1,), (1,)), ((), ())),
                                preferred_element_type=f32)
 
     def wait_for(ref, sem):
         pltpu.make_async_copy(ref, ref, sem).wait()
 
-    stats_box[0] = meta[0:2]
     weigh(0)
 
     def own(j, carry):
@@ -183,14 +190,13 @@
     groups = [[order(i) for i in range(1, nz)][k:k + 4] for k in range(0, nz - 1, 4)]
 
     def next_round(j, carry):
-        add_group(j, groups[0])
-
-        @pl.when(j > 0)
+        for group in groups:
+            add_group(j, group)
+
+        @pl.when(j < ny - 1)
         def _():
-            to_owner(j - 1).start()
-
-        for group in groups[1:]:
-            add_group(j, group)
+            to_owner(j).start()
+
         return carry
 
     lax.fori_loop(0, ny, next_round, 0)
@@ -218,35 +224,27 @@
                       - total_grad * total_grad / (total_hess + l2_penalty))
         best.append(jnp.max(jnp.where(lane < BINS - 1, gain, low), axis=1, keepdims=True))
     half = sc // 2
+    diagonal = iota((node_count, LANES), 0) == iota((node_count, LANES), 1)
+
+    def across(column):
+        return jnp.max(jnp.where(diagonal, column, low), axis=0, keepdims=True)
+
+    top[...] = across(functools.reduce(jnp.maximum, best))
     for s in range(half):
-        best_out[:, s:s + 1] = jnp.where(core == 0, best[s], best[half + s])
-    column = functools.reduce(jnp.maximum, best)
-    diagonal = iota((node_count, LANES), 0) == iota((node_count, LANES), 1)
-    top[...] = jnp.max(jnp.where(diagonal, column, low), axis=0, keepdims=True)
-
-    copies = []
-    for d in range(1, nz):
-        copy = remote(top, top_z.at[d - 1], tz_send.at[d - 1], tz_recv.at[d - 1], at_z(d))
-        copy.start()
-        copies.append(copy)
-    for copy in copies:
-        copy.wait_recv()
-    highest = top[...]
-    for d in range(1, nz):
-        highest = jnp.maximum(highest, top_z[d - 1])
-    mid[...] = highest
-    for i, (dx, dy) in enumerate(xy):
-        copy = remote(mid, top_xy.at[i], txy_send.at[i], txy_recv.at[i], at_xy(dx, dy))
-        copy.start()
-        copies.append(copy)
-    for copy in copies[nz - 1:]:
-        copy.wait_recv()
-    for i in range(len(xy)):
-        highest = jnp.maximum(highest, top_xy[i])
-    node_best_out[...] = highest[:, :node_count]
-
-    for copy in copies + side_copies + [swap]:
+        best_out[s:s + 1] = across(jnp.where(core == 0, best[s], best[half + s]))[:, :node_count]
+
+    others = [(dx, dy, dz) for dx in range(nx) for dy in range(ny) for dz in range(nz)][1:]
+    far = {n: [min(k, n - k) for k in range(n)] for n in (nx, ny, nz)}
+    others.sort(key=lambda d: -(far[nx][d[0]] + far[ny][d[1]] + far[nz][d[2]]))
+    for i, (dx, dy, dz) in enumerate(others):
+        remote(top, tops.at[i], top_send, top_recv,
+               {"rep": lax.rem(x + dx, nx), "rows_0": lax.rem(y + dy, ny), "rows_1": lax.rem(z + dz, nz)}).start()
+    wait_for(tops, top_recv)
+    node_best_out[...] = jnp.maximum(top[...], jnp.max(tops[...], axis=0))[:, :node_count]
+
+    for copy in side_copies + [swap]:
         copy.wait_send()
+    wait_for(tops, top_send)
     for d in range(1, nz):
         remote(stats, stats_box.at[d], stats_send.at[d], stats_recv.at[d], at_z(d)).wait_send()
         remote(node_box.at[0], node_box.at[d], node_send.at[d], node_recv.at[d], at_z(d)).wait_send()
@@ -262,22 +260,23 @@
     node_count, slots_here = elected.shape
     chunks = rows_here // LANES
     sc = slots_here // (ny * nz)
-    meta = jnp.stack([gradients.astype(f32), hessians.astype(f32), parents.astype(f32)]).reshape(3, chunks, LANES)
+    shape = (chunks, LANES)
     vmem, smem = pl.BlockSpec(memory_space=pltpu.VMEM), pl.BlockSpec(memory_space=pltpu.SMEM)
     dma = pltpu.SemaphoreType.DMA
     nodes, best, node_best = pl.pallas_call(
         functools.partial(kernel, ny, nz, nx, sc),
         out_shape=(
             jax.ShapeDtypeStruct((chunks, LANES), i32),
-            jax.ShapeDtypeStruct((node_count, sc // 2), f32),
+            jax.ShapeDtypeStruct((sc // 2, node_count), f32),
             jax.ShapeDtypeStruct((1, node_count), f32),
         ),
-        in_specs=[smem, smem, vmem, vmem, pl.BlockSpec(memory_space=pl.ANY)],
+        in_specs=[smem, smem, vmem, vmem, vmem, vmem, pl.BlockSpec(memory_space=pl.ANY)],
         out_specs=(vmem, vmem, vmem),
         scratch_shapes=[
             pltpu.VMEM((rows_here, width), i32),
             pltpu.VMEM((chunks, LANES), f32),
             pltpu.VMEM((nx - 1, chunks, LANES), f32),
+            pltpu.VMEM((nz, ny, sc, chunks, LANES), f32),
             pltpu.VMEM((nz, ny, sc, chunks, LANES), f32),
             pltpu.VMEM((ny, nz, sc, chunks, LANES), f32),
             pltpu.VMEM((nz, chunks, LANES), f32),
@@ -288,9 +287,7 @@
             pltpu.VMEM((2 * node_count, sc * BINS), f32),
             pltpu.VMEM((2 * node_count, sc * BINS), f32),
             pltpu.VMEM((1, LANES), f32),
-            pltpu.VMEM((nz - 1, 1, LANES), f32),
-            pltpu.VMEM((1, LANES), f32),
-            pltpu.VMEM((nx * ny - 1, 1, LANES), f32),
+            pltpu.VMEM((nx * ny * nz - 1, 1, LANES), f32),
             dma,
             dma((nx - 1,)), dma((nx - 1,)),
             dma((ny, nz)), dma((ny, nz)),
@@ -298,13 +295,12 @@
             dma((nz,)), dma((nz,)),
             dma((ny - 1,)), dma((ny - 1,)),
             dma, dma,
-            dma((nz - 1,)), dma((nz - 1,)),
-            dma((nx * ny - 1,)), dma((nx * ny - 1,)),
+            dma, dma,
         ],
         compiler_params=pltpu.CompilerParams(collective_id=0, has_side_effects=True),
         name="level",
-    )(split_feature, split_bin, meta, elected, binned)
-    return nodes.reshape(rows_here), best[:, None, :], node_best.reshape(node_count)
+    )(split_feature, split_bin, gradients.reshape(shape), hessians.reshape(shape), parents.reshape(shape), elected, binned)
+    return nodes.reshape(rows_here), best.T[:, None, :], node_best.reshape(node_count)
 
 
 def solution(mesh):

time: 51.1 us -> 45.7 us (0.89)
  Pallas kernels: 46.3 us -> 42.4 us
  other arithmetic: 1.31 us -> 0 us
    pallas_call x1, Pallas kernels: 46.3 us -> 42.4 us  [body(): pl.pallas_call(functools.partial(kernel, ny, nz, nx, sc), out_shape=(jax....]
    pallas_call x1 -> x0, local copies, waits for them, and re-layouts: 1.35 us -> none  [body(): pl.pallas_call(functools.partial(kernel, ny, nz, nx, sc), out_shape=(jax....]
    another operation x3 -> x0, other arithmetic: 1.31 us -> none  [body(): jnp.stack([gradients.astype(f32), hessians.astype(f32), parents.astype(f3...]
    unnamed x10 -> x9, local copies, waits for them, and re-layouts: 1.19 us -> 2.41 us
where the time goes in v3:
time: 45.7 us; the launch traced here: 45.4 us
  Pallas kernels  42.4 us (93%)
  local copies, waits for them, and re-layouts  2.41 us (5%)
  between operations  0.65 us (1%)
    pallas_call x1, Pallas kernels, body(): pl.pallas_call(functools.partial(kernel, ny, nz, nx, sc), out_shape=(jax....  42.4 us
    unnamed x9, local copies, waits for them, and re-layouts  2.41 us

profile of v3, /device:TPU:1, one launch (start us, length us, event | category | flops | bytes accessed | tf_op | source)
XLA Modules:
  0.0 45.4 jit_solution(17573528758823913695)
XLA Ops:
  0.6 42.4 %level.1 = (s32[8,128]{1,0:T(8,128)}, f32[2,32]{1,0:T(2,128)}, f32[1,32]{1,0:T(1,128)}) custom-call(s32[16]{0:T(128)} %split_feature.1, s32[16]{0:T(128)} %split_bin.1, bf16[8,128]{1,0:T(8,128)(2,1)} %bitcast.10, bf16[8,128]{1,0:T(8,128)(2,1)} %bitcast.11, s32[8,128]{1,0:T(8,128)} %bitcast.8, s32[32,128]{1,0:T(8,128)} %elected.1, s32[1024,256]{1,0:T(8,128)} %binned_hbm.1), custom_call_target="tpu_custom_call" | custom-call | tf_op jit(solution)/shard_map/level/pallas_call | solution.py:266
  43.0 0.0 copy-start
  43.0 0.7 %copy-done = s32[8,128]{1,0:T(8,128)S(1)} copy-done((s32[8,128]{1,0:T(8,128)S(1)}, s32[8,128]{1,0:T(8,128)}, u32[]{:S(2)}) %copy-start) | copy-done | bytes 4120
  43.7 0.0 copy-start.1
  43.7 0.6 %copy.13 = s32[1024]{0:T(1024)} copy(s32[1024]{0:T(1024)S(1)} %bitcast.9) | data formatting | bytes 8192
  44.3 0.0 copy-done.1
  44.3 0.0 copy-start.2
  44.3 0.6 %copy.14 = f32[32,1,2]{0,2,1:T(2,128)} copy(f32[32,1,2]{0,2,1:T(2,128)S(1)} %bitcast.12) | data formatting | bytes 512
  44.9 0.0 copy-done.2
  44.9 0.5 %copy.15 = f32[32]{0:T(128)} copy(f32[32]{0:T(128)S(1)} %bitcast.13) | data formatting | bytes 256
Async XLA Ops:
  43.0 0.7 %copy-start = (s32[8,128]{1,0:T(8,128)S(1)}, s32[8,128]{1,0:T(8,128)}, u32[]{:S(2)}) copy-start(s32[8,128]{1,0:T(8,128)} %get-tuple-element.6) | copy-start | bytes 12292
  43.7 0.6 %copy-start.1 = (f32[2,32]{1,0:T(2,128)S(1)}, f32[2,32]{1,0:T(2,128)}, u32[]{:S(2)}) copy-start(f32[2,32]{1,0:T(2,128)} %get-tuple-element.7) | copy-start | bytes 772
  44.3 0.6 %copy-start.2 = (f32[1,32]{1,0:T(1,128)S(1)}, f32[1,32]{1,0:T(1,128)}, u32[]{:S(2)}) copy-start(f32[1,32]{1,0:T(1,128)} %get-tuple-element.8) | copy-start | bytes 388

commit v4 on v3

--- a/solution.py
+++ b/solution.py
@@ -30,11 +30,11 @@
     )
 
 
-def kernel(ny, nz, nx, sc, split_feature, split_bin, gradients, hessians, parents, elected, binned_hbm,
+def kernel(ny, nz, nx, sc, split_feature_hbm, split_bin_hbm, gradients_hbm, hessians_hbm, parents_hbm, elected_hbm, binned_hbm,
            nodes_out, best_out, node_best_out,
-           binned, side, side_in, left_box, outbox, zbox, node_box, stats_box, weights, acc, acc_y, mine, acc_in,
+           split_feature, split_bin, gradients, hessians, parents, elected, binned, side, side_in, left_box, outbox, zbox, node_box, stats_box, weights, acc, acc_y, mine, acc_in,
            top, tops,
-           load_sem, side_send, side_recv, z_send, z_recv, node_send, node_recv, stats_send, stats_recv,
+           load_sems, side_send, side_recv, z_send, z_recv, node_send, node_recv, stats_send, stats_recv,
            y_send, y_recv, core_send, core_recv, top_send, top_recv):
     y, z = lax.axis_index("rows_0"), lax.axis_index("rows_1")
     core, x = lax.axis_index("rows_2"), lax.axis_index("rep")
@@ -43,8 +43,11 @@
     width = binned.shape[1]
     chunks = parents.shape[0]
 
-    load = pltpu.make_async_copy(binned_hbm, binned, load_sem)
-    load.start()
+    pairs = ((binned_hbm, binned), (parents_hbm, parents), (split_feature_hbm, split_feature), (split_bin_hbm, split_bin),
+             (gradients_hbm, gradients), (hessians_hbm, hessians), (elected_hbm, elected))
+    loads = [pltpu.make_async_copy(src, dst, load_sems.at[i]) for i, (src, dst) in enumerate(pairs)]
+    for load in loads:
+        load.start()
 
     def at_x(d):
         return {"rep": lax.rem(x + d, nx)}
@@ -53,7 +56,7 @@
         return {"rows_0": lax.rem(y + d, ny)}
 
     def at_z(d):
-        return {"rows_1": lax.rem(z + d, nz)}
+        return {"rows_1": lax.rem(z + d, nz), "rows_2": 1 - core}
 
     def at_xy(dx, dy):
         return {"rep": lax.rem(x + dx, nx), "rows_0": lax.rem(y + dy, ny)}
@@ -68,11 +71,11 @@
     for peer in peers:
         pl.semaphore_signal(barrier, inc=1, device_id=peer, device_id_type=MESH_IDS)
 
+    for load in loads[1:]:
+        load.wait()
     stats_box[0, 0] = gradients[...].astype(f32)
     stats_box[0, 1] = hessians[...].astype(f32)
     parent = parents[...].astype(f32)
-
-    load.wait()
     parent_rows = iota((parent_count, LANES), 0)
     want = jnp.zeros((parent_count, width), i32)
     bound = jnp.zeros((parent_count, LANES), i32)
@@ -81,6 +84,7 @@
         bound = jnp.where(parent_rows == p, split_bin[p], bound)
     pick = jnp.where(iota((parent_count, width), 1) == want, jnp.ones((), f32), jnp.zeros((), f32)).astype(bf16)
     owned = (want[:, :LANES] >= 0) & (want[:, :LANES] < width)
+    loads[0].wait()
     values = lax.dot_general(pick, binned[...].astype(f32).astype(bf16), (((1,), (1,)), ((), ())),
                              preferred_element_type=f32)
     bound = bound.astype(f32)
@@ -170,15 +174,6 @@
 
     lax.fori_loop(0, ny, own, 0)
 
-    def weigh_next(i, carry):
-        d = order(i)
-        wait_for(stats_box.at[d], stats_recv.at[d])
-        wait_for(node_box.at[d], node_recv.at[d])
-        weigh(d)
-        return carry
-
-    lax.fori_loop(1, nz, weigh_next, 0)
-
     def to_owner(j):
         return remote(acc.at[j], acc_y.at[j], y_send.at[j], y_recv.at[j], at_y(1 + j))
 
@@ -187,11 +182,18 @@
             wait_for(zbox.at[j, d], z_recv.at[j, d])
         acc[j] += functools.reduce(jnp.add, [counted(zbox.at[j, d], d) for d in group])
 
-    groups = [[order(i) for i in range(1, nz)][k:k + 4] for k in range(0, nz - 1, 4)]
+    ranked = [order(i) for i in range(1, nz)]
+    for k in range(0, nz - 1, 2):
+        for d in ranked[k:k + 2]:
+            wait_for(stats_box.at[d], stats_recv.at[d])
+            wait_for(node_box.at[d], node_recv.at[d])
+            weigh(d)
+        add_group(0, ranked[k:k + 2])
+    to_owner(0).start()
 
     def next_round(j, carry):
-        for group in groups:
-            add_group(j, group)
+        for k in range(0, nz - 1, 4):
+            add_group(j, ranked[k:k + 4])
 
         @pl.when(j < ny - 1)
         def _():
@@ -199,7 +201,7 @@
 
         return carry
 
-    lax.fori_loop(0, ny, next_round, 0)
+    lax.fori_loop(1, ny, next_round, 0)
     total = acc[ny - 1]
     for j in range(ny - 1):
         to_owner(j).wait_recv()
@@ -238,7 +240,8 @@
     others.sort(key=lambda d: -(far[nx][d[0]] + far[ny][d[1]] + far[nz][d[2]]))
     for i, (dx, dy, dz) in enumerate(others):
         remote(top, tops.at[i], top_send, top_recv,
-               {"rep": lax.rem(x + dx, nx), "rows_0": lax.rem(y + dy, ny), "rows_1": lax.rem(z + dz, nz)}).start()
+               {"rep": lax.rem(x + dx, nx), "rows_0": lax.rem(y + dy, ny), "rows_1": lax.rem(z + dz, nz),
+                "rows_2": 1 - core}).start()
     wait_for(tops, top_recv)
     node_best_out[...] = jnp.maximum(top[...], jnp.max(tops[...], axis=0))[:, :node_count]
 
@@ -254,6 +257,12 @@
         to_owner(j).wait_send()
 
 
+def finish(nodes, best, node_best, nodes_out, best_out, node_best_out):
+    nodes_out[...] = nodes[...]
+    best_out[...] = best[...]
+    node_best_out[...] = node_best[...]
+
+
 def body(sizes, binned, gradients, hessians, parents, split_feature, split_bin, elected):
     ny, nz, nx = sizes
     rows_here, width = binned.shape
@@ -261,18 +270,25 @@
     chunks = rows_here // LANES
     sc = slots_here // (ny * nz)
     shape = (chunks, LANES)
-    vmem, smem = pl.BlockSpec(memory_space=pltpu.VMEM), pl.BlockSpec(memory_space=pltpu.SMEM)
+    vmem = pl.BlockSpec(memory_space=pltpu.VMEM)
     dma = pltpu.SemaphoreType.DMA
-    nodes, best, node_best = pl.pallas_call(
+    results = (
+        jax.ShapeDtypeStruct((chunks, LANES), i32),
+        jax.ShapeDtypeStruct((sc // 2, node_count), f32),
+        jax.ShapeDtypeStruct((1, node_count), f32),
+    )
+    outs = pl.pallas_call(
         functools.partial(kernel, ny, nz, nx, sc),
-        out_shape=(
-            jax.ShapeDtypeStruct((chunks, LANES), i32),
-            jax.ShapeDtypeStruct((sc // 2, node_count), f32),
-            jax.ShapeDtypeStruct((1, node_count), f32),
-        ),
-        in_specs=[smem, smem, vmem, vmem, vmem, vmem, pl.BlockSpec(memory_space=pl.ANY)],
+        out_shape=results,
+        in_specs=[pl.BlockSpec(memory_space=pl.ANY)] * 7,
         out_specs=(vmem, vmem, vmem),
         scratch_shapes=[
+            pltpu.SMEM(split_feature.shape, i32),
+            pltpu.SMEM(split_bin.shape, i32),
+            pltpu.VMEM(shape, bf16),
+            pltpu.VMEM(shape, bf16),
+            pltpu.VMEM(shape, i32),
+            pltpu.VMEM(elected.shape, i32),
             pltpu.VMEM((rows_here, width), i32),
             pltpu.VMEM((chunks, LANES), f32),
             pltpu.VMEM((nx - 1, chunks, LANES), f32),
@@ -288,7 +304,7 @@
             pltpu.VMEM((2 * node_count, sc * BINS), f32),
             pltpu.VMEM((1, LANES), f32),
             pltpu.VMEM((nx * ny * nz - 1, 1, LANES), f32),
-            dma,
+            dma((7,)),
             dma((nx - 1,)), dma((nx - 1,)),
             dma((ny, nz)), dma((ny, nz)),
             dma((nz,)), dma((nz,)),
@@ -300,6 +316,9 @@
         compiler_params=pltpu.CompilerParams(collective_id=0, has_side_effects=True),
         name="level",
     )(split_feature, split_bin, gradients.reshape(shape), hessians.reshape(shape), parents.reshape(shape), elected, binned)
+    nodes, best, node_best = pl.pallas_call(
+        finish, out_shape=results, in_specs=[vmem] * 3, out_specs=(vmem,) * 3, name="finish"
+    )(*outs)
     return nodes.reshape(rows_here), best.T[:, None, :], node_best.reshape(node_count)
 
 

time: 45.7 us -> 43.7 us (0.956)
  local copies, waits for them, and re-layouts: 2.41 us -> 0 us
  Pallas kernels: 42.4 us -> 42.9 us
    unnamed x9 -> x0, local copies, waits for them, and re-layouts: 2.41 us -> none
    pallas_call x1 -> x2, Pallas kernels: 42.4 us -> 42.9 us  [the longest x1 41.6 us: body(): pl.pallas_call(functools.partial(kernel, ny, nz, nx, sc), out_shape=resul...]
where the time goes in v4:
time: 43.7 us; the launch traced here: 43.5 us
  Pallas kernels  42.9 us (98%)
  between operations  0.64 us (1%)
    pallas_call x1, Pallas kernels, body(): pl.pallas_call(functools.partial(kernel, ny, nz, nx, sc), out_shape=resul...  41.6 us
    pallas_call x1, Pallas kernels, body(): pl.pallas_call(finish, out_shape=results, in_specs=[vmem] * 3, out_specs=...  1.28 us

profile of v4, /device:TPU:1, one launch (start us, length us, event | category | flops | bytes accessed | tf_op | source)
XLA Modules:
  0.0 43.5 jit_solution(10586338685068350094)
XLA Ops:
  0.6 41.6 %level.1 = (s32[8,128]{1,0:T(8,128)}, f32[2,32]{1,0:T(2,128)}, f32[1,32]{1,0:T(1,128)}) custom-call(s32[16]{0:T(128)} %split_feature_hbm.1, s32[16]{0:T(128)} %split_bin_hbm.1, bf16[8,128]{1,0:T(8,128)(2,1)} %bitcast.9, bf16[8,128]{1,0:T(8,128)(2,1)} %bitcast.10, s32[8,128]{1,0:T(8,128)} %bitcast.8, s32[32,128]{1,0:T(8,128)} %elected_hbm.1, ...), custom_call_target="tpu_custom_call" | custom-call | tf_op jit(solution)/shard_map/level/pallas_call | solution.py:280
  42.2 1.3 %finish.1 = (s32[8,128]{1,0:T(8,128)}, f32[2,32]{1,0:T(2,128)}, f32[1,32]{1,0:T(1,128)}) custom-call(s32[8,128]{1,0:T(8,128)} %get-tuple-element.9.nodes, f32[2,32]{1,0:T(2,128)} %get-tuple-element.10.best, f32[1,32]{1,0:T(1,128)} %get-tuple-element.11.node_best), custom_call_target="tpu_custom_call" | custom-call | tf_op jit(solution)/shard_map/finish/pallas_call | solution.py:319

commit v5 on v4

--- a/solution.py
+++ b/solution.py
@@ -34,7 +34,7 @@
            nodes_out, best_out, node_best_out,
            split_feature, split_bin, gradients, hessians, parents, elected, binned, side, side_in, left_box, outbox, zbox, node_box, stats_box, weights, acc, acc_y, mine, acc_in,
            top, tops,
-           load_sems, side_send, side_recv, z_send, z_recv, node_send, node_recv, stats_send, stats_recv,
+           answer, load_sems, side_send, side_recv, z_send, z_recv, node_send, node_recv, stats_send, stats_recv,
            y_send, y_recv, core_send, core_recv, top_send, top_recv):
     y, z = lax.axis_index("rows_0"), lax.axis_index("rows_1")
     core, x = lax.axis_index("rows_2"), lax.axis_index("rep")
@@ -43,33 +43,38 @@
     width = binned.shape[1]
     chunks = parents.shape[0]
 
+    def at_x(d):
+        return {"rep": lax.rem(x + d, nx)}
+
+    def at_y(d):
+        return {"rows_0": lax.rem(y + d, ny)}
+
+    half_z = nz // 2
+    side_z, place_z = z // half_z, z % half_z
+
+    def at_z(k):
+        other = k // half_z
+        base = (side_z + other - 2 * side_z * other) * half_z
+        return {"rows_1": base + (place_z + k) % half_z, "rows_2": 1 - core}
+
+    near = [1 + (i // 2 if i % 2 == 0 else half_z - 2 - i // 2) for i in range(half_z - 1)]
+    across = [half_z + k for k in ([1 + (i // 2 if i % 2 == 0 else half_z - 2 - i // 2) for i in range(half_z - 1)] + [0])]
+    core_mate = {"rows_2": 1 - core}
+    beside = [at_x(d) for d in range(1, nx)] + [at_y(d) for d in range(1, ny)] + [core_mate] + [at_z(k) for k in near]
+    barrier = pltpu.get_barrier_semaphore()
+    for peer in beside:
+        pl.semaphore_signal(barrier, inc=1, device_id=peer, device_id_type=MESH_IDS)
+
+    @pl.when(side_z == 0)
+    def _():
+        for k in across:
+            pl.semaphore_signal(barrier, inc=1, device_id=at_z(k), device_id_type=MESH_IDS)
+
     pairs = ((binned_hbm, binned), (parents_hbm, parents), (split_feature_hbm, split_feature), (split_bin_hbm, split_bin),
              (gradients_hbm, gradients), (hessians_hbm, hessians), (elected_hbm, elected))
     loads = [pltpu.make_async_copy(src, dst, load_sems.at[i]) for i, (src, dst) in enumerate(pairs)]
     for load in loads:
         load.start()
-
-    def at_x(d):
-        return {"rep": lax.rem(x + d, nx)}
-
-    def at_y(d):
-        return {"rows_0": lax.rem(y + d, ny)}
-
-    def at_z(d):
-        return {"rows_1": lax.rem(z + d, nz), "rows_2": 1 - core}
-
-    def at_xy(dx, dy):
-        return {"rep": lax.rem(x + dx, nx), "rows_0": lax.rem(y + dy, ny)}
-
-    def order(i):
-        half, odd = (i + 1) // 2, i % 2
-        return (odd * half + (1 - odd) * (nz - half)) % nz
-
-    xy = [(dx, dy) for dx in range(nx) for dy in range(ny) if (dx, dy) != (0, 0)]
-    peers = [at_z(d) for d in range(1, nz)] + [at_xy(*d) for d in xy] + [{"rows_2": 1 - core}]
-    barrier = pltpu.get_barrier_semaphore()
-    for peer in peers:
-        pl.semaphore_signal(barrier, inc=1, device_id=peer, device_id_type=MESH_IDS)
 
     for load in loads[1:]:
         load.wait()
@@ -92,16 +97,43 @@
         hit = (parent_rows.astype(f32) == parent[c:c + 1]) & owned & (values[:, c * LANES:(c + 1) * LANES] > bound)
         side[c:c + 1, :] = jnp.max(jnp.where(hit, 1.0, 0.0), axis=0, keepdims=True)
 
-    pl.semaphore_wait(barrier, len(peers))
+    pl.semaphore_wait(barrier, len(beside) + side_z * len(across))
+
+    @pl.when(side_z == 1)
+    def _():
+        for k in across:
+            pl.semaphore_signal(answer, inc=1, device_id=at_z(k), device_id_type=MESH_IDS)
+
     side_copies = []
     for d in range(1, nx):
         copy = remote(side, side_in.at[d - 1], side_send.at[d - 1], side_recv.at[d - 1], at_x(d))
         copy.start()
         side_copies.append(copy)
-    stats = stats_box.at[0]
-    for i in range(1, nz):
-        d = order(i)
-        remote(stats, stats_box.at[d], stats_send.at[d], stats_recv.at[d], at_z(d)).start()
+    def stats_to(k):
+        return remote(stats_box.at[0], stats_box.at[k], stats_send.at[k], stats_recv.at[k], at_z(k))
+
+    def node_to(k):
+        return remote(node_box.at[0], node_box.at[k], node_send.at[k], node_recv.at[k], at_z(k))
+
+    def bins_to(j, k):
+        there = lax.rem(y + 1 + j, ny)
+        return remote(outbox.at[at_z(k)["rows_1"], there], zbox.at[j, k], z_send.at[j, k], z_recv.at[j, k], at_z(k))
+
+    def send(ks):
+        for k in ks:
+            node_to(k).start()
+        for j in range(ny):
+            for k in ks:
+                bins_to(j, k).start()
+
+    for k in near:
+        stats_to(k).start()
+
+    @pl.when(side_z == 1)
+    def _():
+        for k in across:
+            stats_to(k).start()
+
     chosen = elected[...].astype(f32).astype(bf16)
     node_rows = iota((node_count, LANES), 0).astype(f32)
     for c in range(chunks):
@@ -132,17 +164,13 @@
     for yy in range(ny):
         for zz in range(nz):
             outbox[zz, yy] = jnp.where(right, outbox[zz, yy], left_box[zz, yy])
-    for i in range(1, nz):
-        d = order(i)
-        remote(node_box.at[0], node_box.at[d], node_send.at[d], node_recv.at[d], at_z(d)).start()
-
-    def bins_to(j, d):
-        there = lax.rem(y + 1 + j, ny)
-        return remote(outbox.at[lax.rem(z + d, nz), there], zbox.at[j, d], z_send.at[j, d], z_recv.at[j, d], at_z(d))
-
-    for j in range(ny):
-        for i in range(1, nz):
-            bins_to(j, order(i)).start()
+    @pl.when(side_z == 0)
+    def _():
+        send(near)
+
+    @pl.when(side_z == 1)
+    def _():
+        send(near + across)
 
     def weigh(d):
         node_of = iota((node_count, LANES), 0, bf16)
@@ -174,6 +202,14 @@
 
     lax.fori_loop(0, ny, own, 0)
 
+    @pl.when(side_z == 0)
+    def _():
+        pl.semaphore_wait(answer, len(across))
+        for k in across:
+            stats_to(k).start()
+        send(across)
+
+
     def to_owner(j):
         return remote(acc.at[j], acc_y.at[j], y_send.at[j], y_recv.at[j], at_y(1 + j))
 
@@ -182,18 +218,20 @@
             wait_for(zbox.at[j, d], z_recv.at[j, d])
         acc[j] += functools.reduce(jnp.add, [counted(zbox.at[j, d], d) for d in group])
 
-    ranked = [order(i) for i in range(1, nz)]
-    for k in range(0, nz - 1, 2):
-        for d in ranked[k:k + 2]:
+    ranked = near + across
+    cuts = [0, 2, 3, 5, 6, 7] if nz == 8 else list(range(nz))
+    late_cuts = [0, 4, 6, 7] if nz == 8 else list(range(nz))
+    for lo, hi in zip(cuts, cuts[1:]):
+        for d in ranked[lo:hi]:
             wait_for(stats_box.at[d], stats_recv.at[d])
             wait_for(node_box.at[d], node_recv.at[d])
             weigh(d)
-        add_group(0, ranked[k:k + 2])
+        add_group(0, ranked[lo:hi])
     to_owner(0).start()
 
     def next_round(j, carry):
-        for k in range(0, nz - 1, 4):
-            add_group(j, ranked[k:k + 4])
+        for lo, hi in zip(late_cuts, late_cuts[1:]):
+            add_group(j, ranked[lo:hi])
 
         @pl.when(j < ny - 1)
         def _():
@@ -208,7 +246,7 @@
         total = total + acc_y[j]
     mine[...] = total
 
-    swap = remote(mine, acc_in, core_send, core_recv, {"rows_2": 1 - core})
+    swap = remote(mine, acc_in, core_send, core_recv, core_mate)
     swap.start()
     swap.wait_recv()
     hist = total + acc_in[...]
@@ -228,12 +266,12 @@
     half = sc // 2
     diagonal = iota((node_count, LANES), 0) == iota((node_count, LANES), 1)
 
-    def across(column):
+    def spread(column):
         return jnp.max(jnp.where(diagonal, column, low), axis=0, keepdims=True)
 
-    top[...] = across(functools.reduce(jnp.maximum, best))
+    top[...] = spread(functools.reduce(jnp.maximum, best))
     for s in range(half):
-        best_out[s:s + 1] = across(jnp.where(core == 0, best[s], best[half + s]))[:, :node_count]
+        best_out[s:s + 1] = spread(jnp.where(core == 0, best[s], best[half + s]))[:, :node_count]
 
     others = [(dx, dy, dz) for dx in range(nx) for dy in range(ny) for dz in range(nz)][1:]
     far = {n: [min(k, n - k) for k in range(n)] for n in (nx, ny, nz)}
@@ -248,19 +286,22 @@
     for copy in side_copies + [swap]:
         copy.wait_send()
     wait_for(tops, top_send)
-    for d in range(1, nz):
-        remote(stats, stats_box.at[d], stats_send.at[d], stats_recv.at[d], at_z(d)).wait_send()
-        remote(node_box.at[0], node_box.at[d], node_send.at[d], node_recv.at[d], at_z(d)).wait_send()
+    for k in range(1, nz):
+        stats_to(k).wait_send()
+        node_to(k).wait_send()
         for j in range(ny):
-            bins_to(j, d).wait_send()
+            bins_to(j, k).wait_send()
     for j in range(ny - 1):
         to_owner(j).wait_send()
 
 
-def finish(nodes, best, node_best, nodes_out, best_out, node_best_out):
-    nodes_out[...] = nodes[...]
-    best_out[...] = best[...]
-    node_best_out[...] = node_best[...]
+def finish(nodes, best, node_best, nodes_out, best_out, node_best_out, sems):
+    pairs = ((nodes, nodes_out), (best, best_out), (node_best, node_best_out))
+    copies = [pltpu.make_async_copy(src, dst, sems.at[i]) for i, (src, dst) in enumerate(pairs)]
+    for copy in copies:
+        copy.start()
+    for copy in copies:
+        copy.wait()
 
 
 def body(sizes, binned, gradients, hessians, parents, split_feature, split_bin, elected):
@@ -270,7 +311,7 @@
     chunks = rows_here // LANES
     sc = slots_here // (ny * nz)
     shape = (chunks, LANES)
-    vmem = pl.BlockSpec(memory_space=pltpu.VMEM)
+    vmem, hbm = pl.BlockSpec(memory_space=pltpu.VMEM), pl.BlockSpec(memory_space=pl.ANY)
     dma = pltpu.SemaphoreType.DMA
     results = (
         jax.ShapeDtypeStruct((chunks, LANES), i32),
@@ -280,7 +321,7 @@
     outs = pl.pallas_call(
         functools.partial(kernel, ny, nz, nx, sc),
         out_shape=results,
-        in_specs=[pl.BlockSpec(memory_space=pl.ANY)] * 7,
+        in_specs=[hbm] * 7,
         out_specs=(vmem, vmem, vmem),
         scratch_shapes=[
             pltpu.SMEM(split_feature.shape, i32),
@@ -304,6 +345,7 @@
             pltpu.VMEM((2 * node_count, sc * BINS), f32),
             pltpu.VMEM((1, LANES), f32),
             pltpu.VMEM((nx * ny * nz - 1, 1, LANES), f32),
+            pltpu.SemaphoreType.REGULAR,
             dma((7,)),
             dma((nx - 1,)), dma((nx - 1,)),
             dma((ny, nz)), dma((ny, nz)),
@@ -317,7 +359,7 @@
         name="level",
     )(split_feature, split_bin, gradients.reshape(shape), hessians.reshape(shape), parents.reshape(shape), elected, binned)
     nodes, best, node_best = pl.pallas_call(
-        finish, out_shape=results, in_specs=[vmem] * 3, out_specs=(vmem,) * 3, name="finish"
+        finish, out_shape=results, in_specs=[hbm] * 3, out_specs=(hbm,) * 3, scratch_shapes=[dma((3,))], name="finish"
     )(*outs)
     return nodes.reshape(rows_here), best.T[:, None, :], node_best.reshape(node_count)
 

time: 43.7 us -> 48.2 us (1.10)
  Pallas kernels: 42.9 us -> 47.5 us
    pallas_call x1, Pallas kernels: 41.6 us -> 46.2 us  [body(): pl.pallas_call(functools.partial(kernel, ny, nz, nx, sc), out_shape=resul...]
where the time goes in v5:
time: 48.2 us; the launch traced here: 48.1 us
  Pallas kernels  47.5 us (99%)
  between operations  0.64 us (1%)
    pallas_call x1, Pallas kernels, body(): pl.pallas_call(functools.partial(kernel, ny, nz, nx, sc), out_shape=resul...  46.2 us
    pallas_call x1, Pallas kernels, body(): pl.pallas_call(finish, out_shape=results, in_specs=[hbm] * 3, out_specs=(...  1.3 us

profile of v5, /device:TPU:1, one launch (start us, length us, event | category | flops | bytes accessed | tf_op | source)
XLA Modules:
  0.0 48.1 jit_solution(13778993580992014653)
XLA Ops:
  0.6 46.2 %level.1 = (s32[8,128]{1,0:T(8,128)}, f32[2,32]{1,0:T(2,128)}, f32[1,32]{1,0:T(1,128)}) custom-call(s32[16]{0:T(128)} %split_feature_hbm.1, s32[16]{0:T(128)} %split_bin_hbm.1, bf16[8,128]{1,0:T(8,128)(2,1)} %bitcast.9, bf16[8,128]{1,0:T(8,128)(2,1)} %bitcast.10, s32[8,128]{1,0:T(8,128)} %bitcast.8, s32[32,128]{1,0:T(8,128)} %elected_hbm.1, ...), custom_call_target="tpu_custom_call" | custom-call | tf_op jit(solution)/shard_map/level/pallas_call | solution.py:321
  46.8 1.3 %finish.1 = (s32[8,128]{1,0:T(8,128)}, f32[2,32]{1,0:T(2,128)}, f32[1,32]{1,0:T(1,128)}) custom-call(s32[8,128]{1,0:T(8,128)} %get-tuple-element.9.nodes, f32[2,32]{1,0:T(2,128)} %get-tuple-element.10.best, f32[1,32]{1,0:T(1,128)} %get-tuple-element.11.node_best), custom_call_target="tpu_custom_call" | custom-call | tf_op jit(solution)/shard_map/finish/pallas_call | solution.py:361

commit v6 on v5

--- a/solution.py
+++ b/solution.py
@@ -49,26 +49,24 @@
     def at_y(d):
         return {"rows_0": lax.rem(y + d, ny)}
 
+    def at_z(d):
+        return {"rows_1": lax.rem(z + d, nz), "rows_2": 1 - core}
+
     half_z = nz // 2
     side_z, place_z = z // half_z, z % half_z
-
-    def at_z(k):
-        other = k // half_z
-        base = (side_z + other - 2 * side_z * other) * half_z
-        return {"rows_1": base + (place_z + k) % half_z, "rows_2": 1 - core}
-
-    near = [1 + (i // 2 if i % 2 == 0 else half_z - 2 - i // 2) for i in range(half_z - 1)]
-    across = [half_z + k for k in ([1 + (i // 2 if i % 2 == 0 else half_z - 2 - i // 2) for i in range(half_z - 1)] + [0])]
+    near = [{"rows_1": side_z * half_z + (place_z + k) % half_z, "rows_2": 1 - core} for k in range(1, half_z)]
+    across = [{"rows_1": (1 - side_z) * half_z + (place_z + k) % half_z, "rows_2": 1 - core} for k in range(half_z)]
     core_mate = {"rows_2": 1 - core}
-    beside = [at_x(d) for d in range(1, nx)] + [at_y(d) for d in range(1, ny)] + [core_mate] + [at_z(k) for k in near]
+    beside = [at_x(d) for d in range(1, nx)] + [at_y(d) for d in range(1, ny)] + [core_mate] + near
+    ranked = [(i + 1) // 2 if i % 2 else nz - i // 2 for i in range(1, nz)]
     barrier = pltpu.get_barrier_semaphore()
     for peer in beside:
         pl.semaphore_signal(barrier, inc=1, device_id=peer, device_id_type=MESH_IDS)
 
     @pl.when(side_z == 0)
     def _():
-        for k in across:
-            pl.semaphore_signal(barrier, inc=1, device_id=at_z(k), device_id_type=MESH_IDS)
+        for peer in across:
+            pl.semaphore_signal(barrier, inc=1, device_id=peer, device_id_type=MESH_IDS)
 
     pairs = ((binned_hbm, binned), (parents_hbm, parents), (split_feature_hbm, split_feature), (split_bin_hbm, split_bin),
              (gradients_hbm, gradients), (hessians_hbm, hessians), (elected_hbm, elected))
@@ -101,8 +99,8 @@
 
     @pl.when(side_z == 1)
     def _():
-        for k in across:
-            pl.semaphore_signal(answer, inc=1, device_id=at_z(k), device_id_type=MESH_IDS)
+        for peer in across:
+            pl.semaphore_signal(answer, inc=1, device_id=peer, device_id_type=MESH_IDS)
 
     side_copies = []
     for d in range(1, nx):
@@ -119,20 +117,18 @@
         there = lax.rem(y + 1 + j, ny)
         return remote(outbox.at[at_z(k)["rows_1"], there], zbox.at[j, k], z_send.at[j, k], z_recv.at[j, k], at_z(k))
 
-    def send(ks):
-        for k in ks:
+    def send_stats():
+        for k in ranked:
+            stats_to(k).start()
+
+    def send_rows():
+        for k in ranked:
             node_to(k).start()
         for j in range(ny):
-            for k in ks:
+            for k in ranked:
                 bins_to(j, k).start()
 
-    for k in near:
-        stats_to(k).start()
-
-    @pl.when(side_z == 1)
-    def _():
-        for k in across:
-            stats_to(k).start()
+    pl.when(side_z == 1)(send_stats)
 
     chosen = elected[...].astype(f32).astype(bf16)
     node_rows = iota((node_count, LANES), 0).astype(f32)
@@ -164,13 +160,7 @@
     for yy in range(ny):
         for zz in range(nz):
             outbox[zz, yy] = jnp.where(right, outbox[zz, yy], left_box[zz, yy])
-    @pl.when(side_z == 0)
-    def _():
-        send(near)
-
-    @pl.when(side_z == 1)
-    def _():
-        send(near + across)
+    pl.when(side_z == 1)(send_rows)
 
     def weigh(d):
         node_of = iota((node_count, LANES), 0, bf16)
@@ -205,10 +195,8 @@
     @pl.when(side_z == 0)
     def _():
         pl.semaphore_wait(answer, len(across))
-        for k in across:
-            stats_to(k).start()
-        send(across)
-
+        send_stats()
+        send_rows()
 
     def to_owner(j):
         return remote(acc.at[j], acc_y.at[j], y_send.at[j], y_recv.at[j], at_y(1 + j))
@@ -218,9 +206,8 @@
             wait_for(zbox.at[j, d], z_recv.at[j, d])
         acc[j] += functools.reduce(jnp.add, [counted(zbox.at[j, d], d) for d in group])
 
-    ranked = near + across
-    cuts = [0, 2, 3, 5, 6, 7] if nz == 8 else list(range(nz))
-    late_cuts = [0, 4, 6, 7] if nz == 8 else list(range(nz))
+    cuts = list(range(0, nz - 1, 2)) + [nz - 1]
+    late_cuts = [0, 4, 6, 7] if nz == 8 else cuts
     for lo, hi in zip(cuts, cuts[1:]):
         for d in ranked[lo:hi]:
             wait_for(stats_box.at[d], stats_recv.at[d])
@@ -295,13 +282,10 @@
         to_owner(j).wait_send()
 
 
-def finish(nodes, best, node_best, nodes_out, best_out, node_best_out, sems):
-    pairs = ((nodes, nodes_out), (best, best_out), (node_best, node_best_out))
-    copies = [pltpu.make_async_copy(src, dst, sems.at[i]) for i, (src, dst) in enumerate(pairs)]
-    for copy in copies:
-        copy.start()
-    for copy in copies:
-        copy.wait()
+def finish(nodes, best, node_best, nodes_out, best_out, node_best_out):
+    nodes_out[...] = nodes[...]
+    best_out[...] = best[...]
+    node_best_out[...] = node_best[...]
 
 
 def body(sizes, binned, gradients, hessians, parents, split_feature, split_bin, elected):
@@ -320,7 +304,7 @@
     )
     outs = pl.pallas_call(
         functools.partial(kernel, ny, nz, nx, sc),
-        out_shape=results,
+        out_shape=tuple(pltpu.VMEM(r.shape, r.dtype) for r in results),
         in_specs=[hbm] * 7,
         out_specs=(vmem, vmem, vmem),
         scratch_shapes=[
@@ -359,8 +343,8 @@
         name="level",
     )(split_feature, split_bin, gradients.reshape(shape), hessians.reshape(shape), parents.reshape(shape), elected, binned)
     nodes, best, node_best = pl.pallas_call(
-        finish, out_shape=results, in_specs=[hbm] * 3, out_specs=(hbm,) * 3, scratch_shapes=[dma((3,))], name="finish"
-    )(*outs)
+        finish, out_shape=results, in_specs=[vmem] * 3, out_specs=(vmem,) * 3, name="finish"
+    )(*(pltpu.with_memory_space_constraint(out, pltpu.VMEM) for out in outs))
     return nodes.reshape(rows_here), best.T[:, None, :], node_best.reshape(node_count)
 
 

time: 48.2 us -> 43.3 us (0.90)
  Pallas kernels: 47.5 us -> 42.6 us
    pallas_call x2, Pallas kernels: 47.5 us -> 42.6 us  [the longest x1 42 us: body(): pl.pallas_call(functools.partial(kernel, ny, nz, nx, sc), out_shape=tuple...]
where the time goes in v6:
time: 43.3 us; the launch traced here: 43.2 us
  Pallas kernels  42.6 us (98%)
  between operations  0.64 us (1%)
    pallas_call x1, Pallas kernels, body(): pl.pallas_call(functools.partial(kernel, ny, nz, nx, sc), out_shape=tuple...  42 us

profile of v6, /device:TPU:1, one launch (start us, length us, event | category | flops | bytes accessed | tf_op | source)
XLA Modules:
  0.0 43.2 jit_solution(12762394862975739366)
XLA Ops:
  0.6 42.0 %level.1 = (s32[8,128]{1,0:T(8,128)S(1)}, f32[2,32]{1,0:T(2,128)S(1)}, f32[1,32]{1,0:T(1,128)S(1)}) custom-call(s32[16]{0:T(128)} %split_feature_hbm.1, s32[16]{0:T(128)} %split_bin_hbm.1, bf16[8,128]{1,0:T(8,128)(2,1)} %bitcast.9, bf16[8,128]{1,0:T(8,128)(2,1)} %bitcast.10, s32[8,128]{1,0:T(8,128)} %bitcast.8, s32[32,128]{1,0:T(8,128)} %elected_hbm.1, ...), custom_call_target="tpu_custom_call" | custom-call | tf_op jit(solution)/shard_map/level/pallas_call | solution.py:305
  42.6 0.6 %finish.1 = (s32[8,128]{1,0:T(8,128)}, f32[2,32]{1,0:T(2,128)}, f32[1,32]{1,0:T(1,128)}) custom-call(s32[8,128]{1,0:T(8,128)S(1)} %get-tuple-element.9.nodes, f32[2,32]{1,0:T(2,128)S(1)} %get-tuple-element.10.best, f32[1,32]{1,0:T(1,128)S(1)} %get-tuple-element.11.node_best), custom_call_target="tpu_custom_call" | custom-call | tf_op jit(solution)/shard_map/finish/pallas_call | solution.py:345

commit v7 on v6

--- a/solution.py
+++ b/solution.py
@@ -34,7 +34,7 @@
            nodes_out, best_out, node_best_out,
            split_feature, split_bin, gradients, hessians, parents, elected, binned, side, side_in, left_box, outbox, zbox, node_box, stats_box, weights, acc, acc_y, mine, acc_in,
            top, tops,
-           answer, load_sems, side_send, side_recv, z_send, z_recv, node_send, node_recv, stats_send, stats_recv,
+           load_sems, side_send, side_recv, z_send, z_recv, node_send, node_recv, stats_send, stats_recv,
            y_send, y_recv, core_send, core_recv, top_send, top_recv):
     y, z = lax.axis_index("rows_0"), lax.axis_index("rows_1")
     core, x = lax.axis_index("rows_2"), lax.axis_index("rep")
@@ -52,21 +52,12 @@
     def at_z(d):
         return {"rows_1": lax.rem(z + d, nz), "rows_2": 1 - core}
 
-    half_z = nz // 2
-    side_z, place_z = z // half_z, z % half_z
-    near = [{"rows_1": side_z * half_z + (place_z + k) % half_z, "rows_2": 1 - core} for k in range(1, half_z)]
-    across = [{"rows_1": (1 - side_z) * half_z + (place_z + k) % half_z, "rows_2": 1 - core} for k in range(half_z)]
     core_mate = {"rows_2": 1 - core}
-    beside = [at_x(d) for d in range(1, nx)] + [at_y(d) for d in range(1, ny)] + [core_mate] + near
-    ranked = [(i + 1) // 2 if i % 2 else nz - i // 2 for i in range(1, nz)]
+    beside = [at_x(d) for d in range(1, nx)] + [at_y(d) for d in range(1, ny)] + [core_mate] + [at_z(d) for d in range(1, nz)]
+    ranked = [4, 1, 7, 3, 5, 2, 6] if nz == 8 else list(range(1, nz))
     barrier = pltpu.get_barrier_semaphore()
     for peer in beside:
         pl.semaphore_signal(barrier, inc=1, device_id=peer, device_id_type=MESH_IDS)
-
-    @pl.when(side_z == 0)
-    def _():
-        for peer in across:
-            pl.semaphore_signal(barrier, inc=1, device_id=peer, device_id_type=MESH_IDS)
 
     pairs = ((binned_hbm, binned), (parents_hbm, parents), (split_feature_hbm, split_feature), (split_bin_hbm, split_bin),
              (gradients_hbm, gradients), (hessians_hbm, hessians), (elected_hbm, elected))
@@ -95,13 +86,7 @@
         hit = (parent_rows.astype(f32) == parent[c:c + 1]) & owned & (values[:, c * LANES:(c + 1) * LANES] > bound)
         side[c:c + 1, :] = jnp.max(jnp.where(hit, 1.0, 0.0), axis=0, keepdims=True)
 
-    pl.semaphore_wait(barrier, len(beside) + side_z * len(across))
-
-    @pl.when(side_z == 1)
-    def _():
-        for peer in across:
-            pl.semaphore_signal(answer, inc=1, device_id=peer, device_id_type=MESH_IDS)
-
+    pl.semaphore_wait(barrier, len(beside))
     side_copies = []
     for d in range(1, nx):
         copy = remote(side, side_in.at[d - 1], side_send.at[d - 1], side_recv.at[d - 1], at_x(d))
@@ -128,7 +113,7 @@
             for k in ranked:
                 bins_to(j, k).start()
 
-    pl.when(side_z == 1)(send_stats)
+    send_stats()
 
     chosen = elected[...].astype(f32).astype(bf16)
     node_rows = iota((node_count, LANES), 0).astype(f32)
@@ -160,7 +145,7 @@
     for yy in range(ny):
         for zz in range(nz):
             outbox[zz, yy] = jnp.where(right, outbox[zz, yy], left_box[zz, yy])
-    pl.when(side_z == 1)(send_rows)
+    send_rows()
 
     def weigh(d):
         node_of = iota((node_count, LANES), 0, bf16)
@@ -191,13 +176,6 @@
         return carry
 
     lax.fori_loop(0, ny, own, 0)
-
-    @pl.when(side_z == 0)
-    def _():
-        pl.semaphore_wait(answer, len(across))
-        send_stats()
-        send_rows()
-
     def to_owner(j):
         return remote(acc.at[j], acc_y.at[j], y_send.at[j], y_recv.at[j], at_y(1 + j))
 
@@ -329,7 +307,6 @@
             pltpu.VMEM((2 * node_count, sc * BINS), f32),
             pltpu.VMEM((1, LANES), f32),
             pltpu.VMEM((nx * ny * nz - 1, 1, LANES), f32),
-            pltpu.SemaphoreType.REGULAR,
             dma((7,)),
             dma((nx - 1,)), dma((nx - 1,)),
             dma((ny, nz)), dma((ny, nz)),

time: 43.3 us -> 41.9 us (0.968)
  Pallas kernels: 42.6 us -> 41.2 us
    pallas_call x1, Pallas kernels: 42 us -> 40.6 us  [body(): pl.pallas_call(functools.partial(kernel, ny, nz, nx, sc), out_shape=tuple...]
where the time goes in v7:
time: 41.9 us; the launch traced here: 41.8 us
  Pallas kernels  41.2 us (98%)
  between operations  0.64 us (2%)
    pallas_call x1, Pallas kernels, body(): pl.pallas_call(functools.partial(kernel, ny, nz, nx, sc), out_shape=tuple...  40.6 us

profile of v7, /device:TPU:1, one launch (start us, length us, event | category | flops | bytes accessed | tf_op | source)
XLA Modules:
  0.0 41.8 jit_solution(14893950555876643570)
XLA Ops:
  0.6 40.6 %level.1 = (s32[8,128]{1,0:T(8,128)S(1)}, f32[2,32]{1,0:T(2,128)S(1)}, f32[1,32]{1,0:T(1,128)S(1)}) custom-call(s32[16]{0:T(128)} %split_feature_hbm.1, s32[16]{0:T(128)} %split_bin_hbm.1, bf16[8,128]{1,0:T(8,128)(2,1)} %bitcast.9, bf16[8,128]{1,0:T(8,128)(2,1)} %bitcast.10, s32[8,128]{1,0:T(8,128)} %bitcast.8, s32[32,128]{1,0:T(8,128)} %elected_hbm.1, ...), custom_call_target="tpu_custom_call" | custom-call | tf_op jit(solution)/shard_map/level/pallas_call | solution.py:283
  41.2 0.6 %finish.1 = (s32[8,128]{1,0:T(8,128)}, f32[2,32]{1,0:T(2,128)}, f32[1,32]{1,0:T(1,128)}) custom-call(s32[8,128]{1,0:T(8,128)S(1)} %get-tuple-element.9.nodes, f32[2,32]{1,0:T(2,128)S(1)} %get-tuple-element.10.best, f32[1,32]{1,0:T(1,128)S(1)} %get-tuple-element.11.node_best), custom_call_target="tpu_custom_call" | custom-call | tf_op jit(solution)/shard_map/finish/pallas_call | solution.py:322

commit v8 on v7

--- a/solution.py
+++ b/solution.py
@@ -54,7 +54,7 @@
 
     core_mate = {"rows_2": 1 - core}
     beside = [at_x(d) for d in range(1, nx)] + [at_y(d) for d in range(1, ny)] + [core_mate] + [at_z(d) for d in range(1, nz)]
-    ranked = [4, 1, 7, 3, 5, 2, 6] if nz == 8 else list(range(1, nz))
+    ranked = [4, 3, 5, 2, 6, 1, 7] if nz == 8 else list(range(1, nz))
     barrier = pltpu.get_barrier_semaphore()
     for peer in beside:
         pl.semaphore_signal(barrier, inc=1, device_id=peer, device_id_type=MESH_IDS)
@@ -98,9 +98,12 @@
     def node_to(k):
         return remote(node_box.at[0], node_box.at[k], node_send.at[k], node_recv.at[k], at_z(k))
 
-    def bins_to(j, k):
-        there = lax.rem(y + 1 + j, ny)
-        return remote(outbox.at[at_z(k)["rows_1"], there], zbox.at[j, k], z_send.at[j, k], z_recv.at[j, k], at_z(k))
+    part = sc // 2
+
+    def bins_to(h, k):
+        there, lo = lax.rem(y + 1 + h // 2, ny), h % 2 * part
+        return remote(outbox.at[lax.rem(z + k, nz), there, pl.ds(lo, part)], zbox.at[h, k],
+                      z_send.at[h, k], z_recv.at[h, k], at_z(k))
 
     def send_stats():
         for k in ranked:
@@ -109,9 +112,9 @@
     def send_rows():
         for k in ranked:
             node_to(k).start()
-        for j in range(ny):
+        for h in range(2 * ny):
             for k in ranked:
-                bins_to(j, k).start()
+                bins_to(h, k).start()
 
     send_stats()
 
@@ -160,7 +163,7 @@
         bin_rows = iota((BINS, LANES), 0, bf16)
         one, zero = jnp.ones((), bf16), jnp.zeros((), bf16)
         hots = []
-        for s in range(sc):
+        for s in range(part):
             row = [box[s, c:c + 1, :].astype(bf16) for c in range(chunks)]
             hots.append(jnp.concatenate([jnp.where(bin_rows == r, one, zero) for r in row], axis=1))
         return lax.dot_general(weights[d], jnp.concatenate(hots, axis=0).astype(f8), (((1,), (1,)), ((), ())),
@@ -171,21 +174,20 @@
 
     weigh(0)
 
-    def own(j, carry):
-        acc[j] = counted(outbox.at[z, lax.rem(y + 1 + j, ny)], 0)
+    def own(h, carry):
+        acc[h] = counted(outbox.at[z, lax.rem(y + 1 + h // 2, ny), pl.ds(h % 2 * part, part)], 0)
         return carry
 
-    lax.fori_loop(0, ny, own, 0)
-    def to_owner(j):
-        return remote(acc.at[j], acc_y.at[j], y_send.at[j], y_recv.at[j], at_y(1 + j))
-
-    def add_group(j, group):
+    lax.fori_loop(0, 2 * ny, own, 0)
+    def to_owner(h):
+        return remote(acc.at[h], acc_y.at[h], y_send.at[h], y_recv.at[h], at_y(1 + h // 2))
+
+    def add_group(h, group):
         for d in group:
-            wait_for(zbox.at[j, d], z_recv.at[j, d])
-        acc[j] += functools.reduce(jnp.add, [counted(zbox.at[j, d], d) for d in group])
-
-    cuts = list(range(0, nz - 1, 2)) + [nz - 1]
-    late_cuts = [0, 4, 6, 7] if nz == 8 else cuts
+            wait_for(zbox.at[h, d], z_recv.at[h, d])
+        acc[h] += functools.reduce(jnp.add, [counted(zbox.at[h, d], d) for d in group])
+
+    cuts, later = ([0, 2, 4, 6, 7], [0, 7]) if nz == 8 else ([0, nz - 1],) * 2
     for lo, hi in zip(cuts, cuts[1:]):
         for d in ranked[lo:hi]:
             wait_for(stats_box.at[d], stats_recv.at[d])
@@ -194,40 +196,53 @@
         add_group(0, ranked[lo:hi])
     to_owner(0).start()
 
-    def next_round(j, carry):
-        for lo, hi in zip(late_cuts, late_cuts[1:]):
-            add_group(j, ranked[lo:hi])
-
-        @pl.when(j < ny - 1)
+    def next_round(h, carry):
+        for lo, hi in zip(later, later[1:]):
+            add_group(h, ranked[lo:hi])
+
+        @pl.when(h < 2 * ny - 2)
         def _():
-            to_owner(j).start()
+            to_owner(h).start()
 
         return carry
 
-    lax.fori_loop(1, ny, next_round, 0)
-    total = acc[ny - 1]
-    for j in range(ny - 1):
-        to_owner(j).wait_recv()
-        total = total + acc_y[j]
-    mine[...] = total
-
-    swap = remote(mine, acc_in, core_send, core_recv, core_mate)
-    swap.start()
-    swap.wait_recv()
-    hist = total + acc_in[...]
+    lax.fori_loop(1, 2 * ny - 1, next_round, 0)
+
     upto = jnp.where(iota((BINS, BINS), 0) <= iota((BINS, BINS), 1), 1.0, 0.0)
     lane = iota((node_count, BINS), 1)
     low = jnp.full((), -3.0e38, f32)
-    best = []
-    for s in range(sc):
-        left = jnp.dot(hist[:, s * BINS:(s + 1) * BINS], upto, precision=lax.Precision.HIGHEST,
-                       preferred_element_type=f32)
-        left_grad, left_hess = left[:node_count], left[node_count:]
-        total_grad, total_hess = left_grad[:, BINS - 1:], left_hess[:, BINS - 1:]
-        gain = 0.5 * (left_grad * left_grad / (left_hess + l2_penalty)
-                      + (total_grad - left_grad) ** 2 / (total_hess - left_hess + l2_penalty)
-                      - total_grad * total_grad / (total_hess + l2_penalty))
-        best.append(jnp.max(jnp.where(lane < BINS - 1, gain, low), axis=1, keepdims=True))
+
+    def swap(i):
+        return remote(mine.at[i], acc_in.at[i], core_send.at[i], core_recv.at[i], core_mate)
+
+    def collect(i):
+        total = acc[2 * ny - 2 + i]
+        for j in range(ny - 1):
+            to_owner(2 * j + i).wait_recv()
+            total = total + acc_y[2 * j + i]
+        mine[i] = total
+        swap(i).start()
+
+    def best_of(i):
+        swap(i).wait_recv()
+        hist = mine[i] + acc_in[i]
+        found = []
+        for s in range(part):
+            left = jnp.dot(hist[:, s * BINS:(s + 1) * BINS], upto, precision=lax.Precision.HIGHEST,
+                           preferred_element_type=f32)
+            left_grad, left_hess = left[:node_count], left[node_count:]
+            total_grad, total_hess = left_grad[:, BINS - 1:], left_hess[:, BINS - 1:]
+            gain = 0.5 * (left_grad * left_grad / (left_hess + l2_penalty)
+                          + (total_grad - left_grad) ** 2 / (total_hess - left_hess + l2_penalty)
+                          - total_grad * total_grad / (total_hess + l2_penalty))
+            found.append(jnp.max(jnp.where(lane < BINS - 1, gain, low), axis=1, keepdims=True))
+        return found
+
+    collect(0)
+    next_round(2 * ny - 1, 0)
+    collect(1)
+    best = best_of(0)
+    best += best_of(1)
     half = sc // 2
     diagonal = iota((node_count, LANES), 0) == iota((node_count, LANES), 1)
 
@@ -248,16 +263,16 @@
     wait_for(tops, top_recv)
     node_best_out[...] = jnp.maximum(top[...], jnp.max(tops[...], axis=0))[:, :node_count]
 
-    for copy in side_copies + [swap]:
+    for copy in side_copies + [swap(0), swap(1)]:
         copy.wait_send()
     wait_for(tops, top_send)
     for k in range(1, nz):
         stats_to(k).wait_send()
         node_to(k).wait_send()
-        for j in range(ny):
-            bins_to(j, k).wait_send()
-    for j in range(ny - 1):
-        to_owner(j).wait_send()
+        for h in range(2 * ny):
+            bins_to(h, k).wait_send()
+    for h in range(2 * ny - 2):
+        to_owner(h).wait_send()
 
 
 def finish(nodes, best, node_best, nodes_out, best_out, node_best_out):
@@ -297,23 +312,23 @@
             pltpu.VMEM((nx - 1, chunks, LANES), f32),
             pltpu.VMEM((nz, ny, sc, chunks, LANES), f32),
             pltpu.VMEM((nz, ny, sc, chunks, LANES), f32),
-            pltpu.VMEM((ny, nz, sc, chunks, LANES), f32),
+            pltpu.VMEM((2 * ny, nz, sc // 2, chunks, LANES), f32),
             pltpu.VMEM((nz, chunks, LANES), f32),
             pltpu.VMEM((nz, 2, chunks, LANES), f32),
             pltpu.VMEM((nz, 2 * node_count, rows_here), bf16),
-            pltpu.VMEM((ny, 2 * node_count, sc * BINS), f32),
-            pltpu.VMEM((ny - 1, 2 * node_count, sc * BINS), f32),
-            pltpu.VMEM((2 * node_count, sc * BINS), f32),
-            pltpu.VMEM((2 * node_count, sc * BINS), f32),
+            pltpu.VMEM((2 * ny, 2 * node_count, sc * BINS // 2), f32),
+            pltpu.VMEM((2 * ny - 2, 2 * node_count, sc * BINS // 2), f32),
+            pltpu.VMEM((2, 2 * node_count, sc * BINS // 2), f32),
+            pltpu.VMEM((2, 2 * node_count, sc * BINS // 2), f32),
             pltpu.VMEM((1, LANES), f32),
             pltpu.VMEM((nx * ny * nz - 1, 1, LANES), f32),
             dma((7,)),
             dma((nx - 1,)), dma((nx - 1,)),
-            dma((ny, nz)), dma((ny, nz)),
+            dma((2 * ny, nz)), dma((2 * ny, nz)),
             dma((nz,)), dma((nz,)),
             dma((nz,)), dma((nz,)),
-            dma((ny - 1,)), dma((ny - 1,)),
-            dma, dma,
+            dma((2 * ny - 2,)), dma((2 * ny - 2,)),
+            dma((2,)), dma((2,)),
             dma, dma,
         ],
         compiler_params=pltpu.CompilerParams(collective_id=0, has_side_effects=True),

time: 41.9 us -> 41.2 us (0.983)
  Pallas kernels: 41.2 us -> 40.5 us
    pallas_call x1, Pallas kernels: 40.6 us -> 39.9 us  [body(): pl.pallas_call(functools.partial(kernel, ny, nz, nx, sc), out_shape=tuple...]
where the time goes in v8:
time: 41.2 us; the launch traced here: 41.1 us
  Pallas kernels  40.5 us (98%)
  between operations  0.64 us (2%)
    pallas_call x1, Pallas kernels, body(): pl.pallas_call(functools.partial(kernel, ny, nz, nx, sc), out_shape=tuple...  39.9 us

profile of v8, /device:TPU:1, one launch (start us, length us, event | category | flops | bytes accessed | tf_op | source)
XLA Modules:
  0.0 41.1 jit_solution(3285731806370467055)
XLA Ops:
  0.6 39.9 %level.1 = (s32[8,128]{1,0:T(8,128)S(1)}, f32[2,32]{1,0:T(2,128)S(1)}, f32[1,32]{1,0:T(1,128)S(1)}) custom-call(s32[16]{0:T(128)} %split_feature_hbm.1, s32[16]{0:T(128)} %split_bin_hbm.1, bf16[8,128]{1,0:T(8,128)(2,1)} %bitcast.9, bf16[8,128]{1,0:T(8,128)(2,1)} %bitcast.10, s32[8,128]{1,0:T(8,128)} %bitcast.8, s32[32,128]{1,0:T(8,128)} %elected_hbm.1, ...), custom_call_target="tpu_custom_call" | custom-call | tf_op jit(solution)/shard_map/level/pallas_call | solution.py:298
  40.5 0.6 %finish.1 = (s32[8,128]{1,0:T(8,128)}, f32[2,32]{1,0:T(2,128)}, f32[1,32]{1,0:T(1,128)}) custom-call(s32[8,128]{1,0:T(8,128)S(1)} %get-tuple-element.9.nodes, f32[2,32]{1,0:T(2,128)S(1)} %get-tuple-element.10.best, f32[1,32]{1,0:T(1,128)S(1)} %get-tuple-element.11.node_best), custom_call_target="tpu_custom_call" | custom-call | tf_op jit(solution)/shard_map/finish/pallas_call | solution.py:337

commit v9 on v8

--- a/solution.py
+++ b/solution.py
@@ -238,8 +238,8 @@
             found.append(jnp.max(jnp.where(lane < BINS - 1, gain, low), axis=1, keepdims=True))
         return found
 
+    next_round(2 * ny - 1, 0)
     collect(0)
-    next_round(2 * ny - 1, 0)
     collect(1)
     best = best_of(0)
     best += best_of(1)

time: 41.2 us -> 41.2 us (level)
  no operation moved by 1% of the time
where the time goes in v9:
time: 41.2 us; the launch traced here: 41.1 us
  Pallas kernels  40.4 us (98%)
  between operations  0.64 us (2%)
    pallas_call x1, Pallas kernels, body(): pl.pallas_call(functools.partial(kernel, ny, nz, nx, sc), out_shape=tuple...  39.8 us

profile of v9, /device:TPU:1, one launch (start us, length us, event | category | flops | bytes accessed | tf_op | source)
XLA Modules:
  0.0 41.1 jit_solution(5569439652653460200)
XLA Ops:
  0.6 39.8 %level.1 = (s32[8,128]{1,0:T(8,128)S(1)}, f32[2,32]{1,0:T(2,128)S(1)}, f32[1,32]{1,0:T(1,128)S(1)}) custom-call(s32[16]{0:T(128)} %split_feature_hbm.1, s32[16]{0:T(128)} %split_bin_hbm.1, bf16[8,128]{1,0:T(8,128)(2,1)} %bitcast.9, bf16[8,128]{1,0:T(8,128)(2,1)} %bitcast.10, s32[8,128]{1,0:T(8,128)} %bitcast.8, s32[32,128]{1,0:T(8,128)} %elected_hbm.1, ...), custom_call_target="tpu_custom_call" | custom-call | tf_op jit(solution)/shard_map/level/pallas_call | solution.py:298
  40.5 0.6 %finish.1 = (s32[8,128]{1,0:T(8,128)}, f32[2,32]{1,0:T(2,128)}, f32[1,32]{1,0:T(1,128)}) custom-call(s32[8,128]{1,0:T(8,128)S(1)} %get-tuple-element.9.nodes, f32[2,32]{1,0:T(2,128)S(1)} %get-tuple-element.10.best, f32[1,32]{1,0:T(1,128)S(1)} %get-tuple-element.11.node_best), custom_call_target="tpu_custom_call" | custom-call | tf_op jit(solution)/shard_map/finish/pallas_call | solution.py:337
